TPU v7x, 128 devices: a whole 4x4x4 slice. The times are simulated.
128 devices in a mesh: row: 32 (over z, y_lo, x), col: 4 (over y_hi, core).
Axes of the slice: x: 4, y: 4 (y_hi: 2, y_lo: 2; y = y_hi * 2 + y_lo), z: 4, core: 2. Of those that a mesh axis runs over, the one named last changes fastest.
Arguments:
- voltage: float32 [2, 4096, 16384], P(None, ('row', 'col')), may hold values from -6 to 6
- chirp_phase: float32 [16384, 4096], P(('row', 'col')), may hold values from -3.140625 to 3.140625
- filter_taps: float32 [8, 1024], replicated, may hold values from -0.0625 to 0.0625
Outputs:
- filterbank: float32 [2, 1024, 65536], P(None, None, ('row', 'col'))
All inputs are finite; a program needn't handle non-finite values.
Results may differ from a plain program's by a relative error of at most 0.00015.
Values sent between devices are 32-bit elements; how exact they have to be, the bound alone decides.
A program may use at most 128 MiB of HBM per device.

v0:
```python
import math

import jax
import jax.numpy as jnp
from jax import lax
from jax.sharding import PartitionSpec as P

precise = lax.Precision.HIGHEST


def split_up(x, dim, size):
    dims = x.shape
    pieces = x.reshape(*dims[:dim], size, dims[dim] // size, *dims[dim + 1 :])
    return jnp.moveaxis(pieces, dim, 0)


def laid_out(pieces, dim):
    pieces = jnp.moveaxis(pieces, 0, dim)
    dims = pieces.shape
    return pieces.reshape(*dims[:dim], dims[dim] * dims[dim + 1], *dims[dim + 2 :])


def joined_exchange(x, axis, axes, splits, concats):
    sizes = [lax.axis_size(a) for a in axes]
    pieces = split_up(x, splits[0], sizes[0])
    pieces = jnp.moveaxis(split_up(pieces, splits[1] + 1, sizes[1]), 0, 1)
    inside = pieces.shape[2:]
    pieces = pieces.reshape(-1, *inside)
    pieces = lax.all_to_all(pieces, axis, split_axis=0, concat_axis=0, tiled=True)
    pieces = laid_out(pieces.reshape(*sizes, *inside), concats[0] + 1)
    return laid_out(pieces, concats[1])


def passed_along(block, axis, distance):
    devices = range(lax.axis_size(axis))
    route = [(i - distance, i) for i in devices if i - distance in devices]
    return lax.ppermute(block, axis, route)


def dft_table(radix, direction):
    digits = jnp.arange(radix, dtype=jnp.int32)
    product = digits[:, None] * digits[None, :] % radix
    turn = direction * 2.0 * math.pi / radix * product.astype(jnp.float32)
    cos_part = jnp.cos(turn)
    sin_part = jnp.sin(turn)
    upper = jnp.stack([cos_part, sin_part], axis=1)
    lower = jnp.stack([-sin_part, cos_part], axis=1)
    return jnp.stack([upper, lower], axis=0)


def complex_product(values, cos_part, sin_part):
    real_part = values[0] * cos_part - values[1] * sin_part
    imag_part = values[0] * sin_part + values[1] * cos_part
    return jnp.stack([real_part, imag_part])


def inner_twist(outer_radix, inner_radix, direction):
    outer_digits = jnp.arange(outer_radix, dtype=jnp.int32)
    inner_digits = jnp.arange(inner_radix, dtype=jnp.int32)
    length = outer_radix * inner_radix
    product = outer_digits[:, None] * inner_digits[None, :] % length
    turn = direction * 2.0 * math.pi / length * product.astype(jnp.float32)
    return (jnp.cos(turn), jnp.sin(turn))


def dft_rows(values, direction):
    length = values.shape[1]
    column_count = values.shape[2]
    inner_radix = min(length, 128)
    outer_radix = length // inner_radix
    blocked = values.reshape(2, outer_radix, inner_radix, column_count)
    partial_value = jnp.einsum(
        "cadk,cabm->dkbm", dft_table(outer_radix, direction), blocked, precision=precise
    )
    cos_part, sin_part = inner_twist(outer_radix, inner_radix, direction)
    partial_value = complex_product(partial_value, cos_part[:, :, None], sin_part[:, :, None])
    result = jnp.einsum(
        "cbdq,ckbm->dqkm", dft_table(inner_radix, direction), partial_value, precision=precise
    )
    return result.reshape(2, length, column_count)


def dft_cols(values, direction):
    length = values.shape[2]
    row_count = values.shape[1]
    inner_radix = min(length, 128)
    outer_radix = length // inner_radix
    blocked = values.reshape(2, row_count, outer_radix, inner_radix)
    partial_value = jnp.einsum(
        "cadk,cmab->dmkb", dft_table(outer_radix, direction), blocked, precision=precise
    )
    cos_part, sin_part = inner_twist(outer_radix, inner_radix, direction)
    partial_value = complex_product(partial_value, cos_part, sin_part)
    result = jnp.einsum(
        "cbdq,cmkb->dmqk", dft_table(inner_radix, direction), partial_value, precision=precise
    )
    return result.reshape(2, row_count, length)


def rotate(values, row_index, col_index, total, direction, factor):
    product = row_index[:, None] * col_index[None, :] % total
    turn = direction * 2.0 * math.pi / total * product.astype(jnp.float32)
    return complex_product(values, factor * jnp.cos(turn), factor * jnp.sin(turn))


def spread(values):
    row_devices = lax.axis_size("row")
    col_devices = lax.axis_size("col")
    depth_rows = values.shape[1]
    span_cols = values.shape[2] // (row_devices * col_devices)
    blocked = values.reshape(2, 1, 1, depth_rows, row_devices, col_devices, span_cols)
    arrived = joined_exchange(blocked, ("row", "col"), ("row", "col"), (4, 5), (1, 2))
    return arrived.reshape(2, row_devices * col_devices * depth_rows, span_cols)


def collect(values):
    row_devices = lax.axis_size("row")
    col_devices = lax.axis_size("col")
    depth_rows = values.shape[1] // (row_devices * col_devices)
    span_cols = values.shape[2]
    blocked = values.reshape(2, row_devices, col_devices, depth_rows, 1, 1, span_cols)
    arrived = joined_exchange(blocked, ("row", "col"), ("row", "col"), (1, 2), (4, 5))
    return arrived.reshape(2, depth_rows, row_devices * col_devices * span_cols)


def local(voltage, chirp_phase, filter_taps):
    device_count = lax.axis_size("row") * lax.axis_size("col")
    device = lax.axis_index(("row", "col"))
    local_rows = voltage.shape[1]
    total_rows = local_rows * device_count
    total_cols = voltage.shape[2]
    local_cols = total_cols // device_count
    total = total_rows * total_cols
    signal = spread(voltage)
    signal = dft_rows(signal, -1.0)
    row_index = jnp.arange(total_rows, dtype=jnp.int32)
    col_index = device * local_cols + jnp.arange(local_cols, dtype=jnp.int32)
    signal = rotate(signal, row_index, col_index, total, -1.0, 1.0)
    signal = collect(signal)
    signal = dft_cols(signal, -1.0)
    turned_phase = jnp.transpose(chirp_phase)
    local_phase = lax.all_to_all(
        turned_phase, ("row", "col"), split_axis=0, concat_axis=1, tiled=True
    )
    signal = complex_product(signal, jnp.cos(local_phase), jnp.sin(local_phase))
    signal = dft_cols(signal, 1.0)
    row_index = device * local_rows + jnp.arange(local_rows, dtype=jnp.int32)
    col_index = jnp.arange(total_cols, dtype=jnp.int32)
    signal = rotate(signal, row_index, col_index, total, 1.0, 1.0 / total)
    signal = spread(signal)
    signal = dft_rows(signal, 1.0)
    signal = collect(signal)
    tap_count = filter_taps.shape[0]
    channel_count = filter_taps.shape[1]
    samples = signal.reshape(2, local_rows * total_cols)
    frame_count = samples.shape[1] // channel_count
    frames = samples.reshape(2, frame_count, channel_count)
    history = passed_along(frames[:, frame_count - tap_count + 1 :, :], ("row", "col"), 1)
    extended = jnp.concatenate([history, frames], axis=1)
    turned = jnp.transpose(extended, (0, 2, 1))
    weighted = jnp.zeros((2, channel_count, frame_count), jnp.float32)
    for tap_delay in range(tap_count):
        offset = tap_count - 1 - tap_delay
        weighted = (
            weighted
            + filter_taps[tap_delay][None, :, None] * turned[:, :, offset : offset + frame_count]
        )
    return dft_rows(weighted, -1.0)


def solution(mesh):
    in_specs = (P(None, ("row", "col"), None), P(("row", "col"), None), P())
    out_specs = P(None, None, ("row", "col"))
    return jax.shard_map(local, mesh=mesh, in_specs=in_specs, out_specs=out_specs, check_vma=False)
```

profile of v0, /device:TPU:1, one launch (start us, length us, event | category | flops | bytes accessed | tf_op | source)
XLA Modules:
  0.0 433.3 jit_solution(13439741225452123835)
XLA Ops:
  0.0 6.0 %reshape_reshape.2 = f32[2,1,1,32,32,1,4,128]{7,6,4,3,0,5,2,1:T(4,128)} reshape(f32[2,32,16384]{2,1,0:T(8,128)} %param.3) | data formatting | bytes 8388608 | tf_op jit(solution)/shard_map/reshape;reshape | solution.py:13
  6.0 6.7 %copy.107 = f32[2,1,1,32,32,1,4,128]{7,3,0,6,4,5,2,1:T(8,128)} copy(f32[2,1,1,32,32,1,4,128]{7,6,4,3,0,5,2,1:T(4,128)} %reshape_reshape.2) | data formatting | bytes 8388608 | tf_op jit(solution)/shard_map/reshape;reshape | solution.py:13
  12.7 11.9 %all-to-all-start = ((f32[128,2,1,1,32,1,1,128]{7,4,1,6,5,3,2,0:T(8,128)}), f32[128,2,1,1,32,1,1,128]{7,4,1,6,5,3,2,0:T(8,128)}, u32[]{:S(2)}, u32[]{:S(2)}) async-start(f32[128,2,1,1,32,1,1,128]{7,4,1,6,5,3,2,0:T(8,128)} %bitcast.252), calls=%async_computation | async-start | bytes 8388608 | tf_op jit(solution)/shard_map/all_to_all | solution.py:29
  27.6 48.4 %all-to-all-done = f32[128,2,1,1,32,1,1,128]{7,4,1,6,5,3,2,0:T(8,128)} async-done(((f32[128,2,1,1,32,1,1,128]{7,4,1,6,5,3,2,0:T(8,128)}), f32[128,2,1,1,32,1,1,128]{7,4,1,6,5,3,2,0:T(8,128)}, u32[]{:S(2)}, u32[]{:S(2)}) %all-to-all-start) | async-done | bytes 4194336 | tf_op jit(solution)/shard_map/all_to_all | solution.py:29
  76.0 6.9 %all-to-all-start.2 = ((f32[128,32,128]{2,1,0:T(8,128)}), f32[128,32,128]{2,1,0:T(8,128)S(1)}, u32[]{:S(2)}, u32[]{:S(2)}) async-start(f32[128,32,128]{2,1,0:T(8,128)} %bitcast.60), calls=%async_computation.2 | async-start | bytes 4194304 | tf_op jit(solution)/shard_map/all_to_all | solution.py:142
  83.0 4.6 %copy.108 = f32[2,32,4,1,32,1,1,128]{7,1,0,4,2,6,5,3:T(8,128)S(1)} copy(f32[2,32,4,1,32,1,1,128]{7,4,0,2,1,6,5,3:T(8,128)} %bitcast.29) | data formatting | bytes 8388608 | tf_op jit(solution)/shard_map/transpose | solution.py:18
  87.6 4.1 convolution_bitcast_fusion.1
  93.7 5.9 %fusion.32 = f32[2,128,32,128]{3,1,2,0:T(8,128)S(1)} fusion(f32[2,32,128,128]{3,1,2,0:T(8,128)S(1)} %pad_maximum_fusion, f32[1,128,2,128]{1,3,0,2:T(8,128)S(1)} %get-tuple-element.32, f32[1,128,2,128]{1,3,0,2:T(8,128)S(1)} %get-tuple-element.31), kind=kOutput, calls=%fused_computation.60 | convolution fusion | flops 3221291008 | bytes 8650752 | tf_op jit(solution)/shard_map/cbdq,ckbm->dqkm/dot_general | solution.py:77
  100.1 18.6 %multiply_subtract_fusion.5 = (f32[1,32,1,4,32,1,1,128]{7,3,1,4,6,5,2,0:T(4,128)S(1)}, f32[1,32,1,4,32,1,1,128]{7,3,1,4,6,5,2,0:T(4,128)S(1)}) fusion(f32[1,32,1,4,32,1,1,128]{7,3,1,4,6,5,2,0:T(4,128)S(1)} %bitcast.261, f32[1,32,1,4,32,1,1,128]{7,3,1,4,6,5,2,0:T(4,128)S(1)} %bitcast.260, s32[128]{0:T(128)S(1)} %iota_add_fusion.1, ...), kind=kLoop, calls=%fused_computation.94 | loop fusion | flops 10485760 | bytes 8405504 | tf_op jit(solution)/shard_map/sub | solution.py:52
  120.7 4.4 %copy.110 = f32[32,4,2,1,1,32,1,1,128]{8,5,2,1,0,7,6,4,3:T(8,128)} copy(f32[32,4,2,1,1,32,1,1,128]{8,1,0,5,2,7,6,4,3:T(4,128)S(1)} %maximum_bitcast_fusion.1) | data formatting | bytes 8388608 | tf_op jit(solution)/shard_map/transpose;transpose | solution.py:26
  126.5 10.2 %all-to-all-start.1 = ((f32[128,2,1,1,32,1,1,128]{7,4,1,6,5,3,2,0:T(8,128)}), f32[128,2,1,1,32,1,1,128]{7,4,1,6,5,3,2,0:T(8,128)}, u32[]{:S(2)}, u32[]{:S(2)}) async-start(f32[128,2,1,1,32,1,1,128]{7,4,1,6,5,3,2,0:T(8,128)} %bitcast.253), calls=%async_computation.1 | async-start | bytes 8388608 | tf_op jit(solution)/shard_map/all_to_all | solution.py:29
  140.0 8.2 %fusion.124 = (f32[128,32,128]{0,2,1:T(8,128)}, f32[128,32,128]{0,2,1:T(8,128)}) fusion(f32[128,32,128]{0,2,1:T(8,128)S(1)} %copy.117), kind=kLoop, calls=%fused_computation.217 | loop fusion | bytes 6291456 | tf_op jit(solution)/shard_map/sin | solution.py:145
  148.2 40.0 %all-to-all-done.1 = f32[128,2,1,1,32,1,1,128]{7,4,1,6,5,3,2,0:T(8,128)} async-done(((f32[128,2,1,1,32,1,1,128]{7,4,1,6,5,3,2,0:T(8,128)}), f32[128,2,1,1,32,1,1,128]{7,4,1,6,5,3,2,0:T(8,128)}, u32[]{:S(2)}, u32[]{:S(2)}) %all-to-all-start.1) | async-done | bytes 4194336 | tf_op jit(solution)/shard_map/all_to_all | solution.py:29
  188.2 10.9 %fusion.35 = f32[2,32,128,128]{2,3,0,1:T(8,128)S(1)} fusion(f32[2,32,128,128,1]{3,1,0,2,4:T(8,128)} %bitcast.48, f32[1,128,2,128]{1,3,0,2:T(8,128)S(1)} %get-tuple-element.32, f32[1,128,2,128]{1,3,0,2:T(8,128)S(1)} %get-tuple-element.31), kind=kOutput, calls=%fused_computation.61 | convolution fusion | flops 3221291008 | bytes 8650752 | tf_op jit(solution)/shard_map/cadk,cmab->dmkb/dot_general | solution.py:89
  199.7 7.1 %fusion.45 = f32[2,32,128,128]{2,3,0,1:T(8,128)S(1)} fusion(f32[1,32,128,128]{2,3,0,1:T(8,128)S(1)} %get-tuple-element.16, f32[1,32,128,128]{2,3,0,1:T(8,128)S(1)} %get-tuple-element.15, f32[1,128,2,128]{1,3,0,2:T(8,128)S(1)} %get-tuple-element.32, f32[1,128,2,128]{1,3,0,2:T(8,128)S(1)} %get-tuple-element.31), kind=kOutput, calls=%fused_computation.65 | convolution fusion | flops 3222339584 | bytes 8650752 | tf_op jit(solution)/shard_map/cbdq,cmkb->dmqk/dot_general | solution.py:94
  217.2 18.0 %multiply_subtract_fusion.2 = (f32[1,1,1,32,32,1,4,128]{7,6,4,3,5,2,1,0:T(4,128)S(1)}, f32[1,1,1,32,32,1,4,128]{7,6,4,3,5,2,1,0:T(4,128)S(1)}) fusion(f32[1,1,1,32,32,1,4,128]{7,6,4,3,5,2,1,0:T(4,128)S(1)} %bitcast.263, f32[1,1,1,32,32,1,4,128]{7,6,4,3,5,2,1,0:T(4,128)S(1)} %bitcast.262, s32[32,4,128]{2,1,0:T(4,128)S(1)} %multiply_add_fusion.8, ...), kind=kLoop, calls=%fused_computation.86 | loop fusion | flops 11534336 | bytes 8454272 | tf_op jit(solution)/shard_map/sub | solution.py:52
  237.2 4.4 %copy.122 = f32[32,4,2,1,1,32,1,1,128]{8,5,2,1,0,7,6,4,3:T(8,128)} copy(f32[32,4,2,1,1,32,1,1,128]{8,1,0,5,2,7,6,4,3:T(4,128)S(1)} %maximum_bitcast_fusion.6) | data formatting | bytes 8388608 | tf_op jit(solution)/shard_map/transpose;transpose | solution.py:26
  241.6 7.7 %all-to-all-start.3 = ((f32[128,2,1,1,32,1,1,128]{7,4,1,6,5,3,2,0:T(8,128)}), f32[128,2,1,1,32,1,1,128]{7,4,1,6,5,3,2,0:T(8,128)}, u32[]{:S(2)}, u32[]{:S(2)}) async-start(f32[128,2,1,1,32,1,1,128]{7,4,1,6,5,3,2,0:T(8,128)} %bitcast.255), calls=%async_computation.3 | async-start | bytes 8388608 | tf_op jit(solution)/shard_map/all_to_all | solution.py:29
  249.8 50.8 %all-to-all-done.3 = f32[128,2,1,1,32,1,1,128]{7,4,1,6,5,3,2,0:T(8,128)} async-done(((f32[128,2,1,1,32,1,1,128]{7,4,1,6,5,3,2,0:T(8,128)}), f32[128,2,1,1,32,1,1,128]{7,4,1,6,5,3,2,0:T(8,128)}, u32[]{:S(2)}, u32[]{:S(2)}) %all-to-all-start.3) | async-done | bytes 4194336 | tf_op jit(solution)/shard_map/all_to_all | solution.py:29
  300.6 4.6 %copy.123 = f32[2,32,4,1,32,1,1,128]{7,1,0,4,2,6,5,3:T(8,128)S(1)} copy(f32[2,32,4,1,32,1,1,128]{7,4,0,2,1,6,5,3:T(8,128)} %bitcast.90) | data formatting | bytes 8388608 | tf_op jit(solution)/shard_map/transpose | solution.py:18
  311.3 5.9 %fusion.22 = f32[2,128,32,128,1]{3,1,4,2,0:T(8,128)S(1)} fusion(f32[2,32,128,128]{3,1,2,0:T(8,128)S(1)} %pad_maximum_fusion.1, f32[2,128,2,128,1]{1,3,2,0,4:T(8,128)S(1)} %get-tuple-element.27), kind=kOutput, calls=%fused_computation.38 | convolution fusion | flops 3221225472 | bytes 8650752 | tf_op jit(solution)/shard_map/cbdq,ckbm->dqkm/dot_general | solution.py:77
  317.2 4.4 %copy.127 = f32[32,4,2,1,1,32,1,1,128]{8,5,2,1,0,7,6,4,3:T(8,128)} copy(f32[32,4,2,1,1,32,1,1,128]{8,1,0,5,2,7,6,4,3:T(4,128)S(1)} %bitcast.251) | data formatting | bytes 8388608 | tf_op jit(solution)/shard_map/transpose;transpose | solution.py:26
  321.6 7.5 %all-to-all-start.4 = ((f32[128,2,1,1,32,1,1,128]{7,4,1,6,5,3,2,0:T(8,128)}), f32[128,2,1,1,32,1,1,128]{7,4,1,6,5,3,2,0:T(8,128)}, u32[]{:S(2)}, u32[]{:S(2)}) async-start(f32[128,2,1,1,32,1,1,128]{7,4,1,6,5,3,2,0:T(8,128)} %bitcast.254), calls=%async_computation.4 | async-start | bytes 8388608 | tf_op jit(solution)/shard_map/all_to_all | solution.py:29
  329.6 50.8 %all-to-all-done.4 = f32[128,2,1,1,32,1,1,128]{7,4,1,6,5,3,2,0:T(8,128)} async-done(((f32[128,2,1,1,32,1,1,128]{7,4,1,6,5,3,2,0:T(8,128)}), f32[128,2,1,1,32,1,1,128]{7,4,1,6,5,3,2,0:T(8,128)}, u32[]{:S(2)}, u32[]{:S(2)}) %all-to-all-start.4) | async-done | bytes 4194336 | tf_op jit(solution)/shard_map/all_to_all | solution.py:29
  380.4 6.9 %copy.210 = f32[32,4,2,1,1,32,1,1,128]{8,1,0,5,2,7,6,4,3:T(4,128)} copy(f32[32,4,2,1,1,32,1,1,128]{8,5,2,1,0,7,6,4,3:T(8,128)} %bitcast.103) | data formatting | bytes 8388608 | tf_op jit(solution)/shard_map/reshape | solution.py:30
  387.3 5.5 %reshape_reshape_reshape_reshape.3 = f32[2,512,1024]{2,1,0:T(8,128)} reshape(f32[2,1,1,32,32,4,1,128]{7,5,4,3,0,6,2,1:T(4,128)} %bitcast.259) | data formatting | bytes 8388608 | tf_op jit(solution)/shard_map/reshape;reshape;reshape;reshape | solution.py:157
  393.6 4.8 %collective-permute-start = (f32[2,7,1024]{2,1,0:T(8,128)S(1)}, f32[2,7,1024]{2,1,0:T(8,128)S(1)}, u32[]{:S(2)}, u32[]{:S(2)}) collective-permute-start(f32[2,7,1024]{2,1,0:T(8,128)S(1)} %slice.168), channel_id=1, source_target_pairs={{0,1},{1,2},{2,3},{3,4},{4,5},{5,6},{6,7},{7,8},{8,9},{9,10},{10,1... | collective-permute-start | bytes 172040 | tf_op jit(solution)/shard_map/ppermute | solution.py:37
  402.4 5.3 %fusion = f32[2,1024,512]{1,2,0:T(8,128)} fusion(f32[2,1024,519]{1,2,0:T(8,128)S(1)} %maximum_bitcast_fusion, f32[1024]{0:T(1024)S(1)} %bitcast.270, f32[1024]{0:T(1024)S(1)} %bitcast.271, f32[1024]{0:T(1024)S(1)} %bitcast.265, f32[1024]{0:T(1024)S(1)} %bitcast.266, f32[1024]{0:T(1024)S(1)} %bitcast.267, f32[1024]{0:T(1024)S(1)} %bitcast.268, ...), kind=kLoop, calls=%fused_computation.2 | loop fusion | flops 15728640 | bytes 37781504 | tf_op jit(solution)/shard_map/add | solution.py:165
  407.7 5.4 %copy.129 = f32[2,1024,512]{2,1,0:T(8,128)} copy(f32[2,1024,512]{1,2,0:T(8,128)} %fusion) | data formatting | bytes 8388608 | tf_op jit(solution)/shard_map/add | solution.py:165
  413.1 8.6 %fusion.38 = f32[2,8,128,512]{3,1,2,0:T(8,128)S(1)} fusion(f32[2,8,128,512]{3,2,1,0:T(8,128)} %bitcast.258, f32[1,8,2,8]{1,3,0,2:T(8,128)S(1)} %copy.105, f32[1,8,2,8]{1,3,0,2:T(8,128)S(1)} %copy.104), kind=kOutput, calls=%fused_computation.62 | convolution fusion | flops 201326848 | bytes 8389632 | tf_op jit(solution)/shard_map/cadk,cabm->dkbm/dot_general | solution.py:72
  422.7 5.9 %fusion.41 = f32[2,128,8,512]{3,1,2,0:T(8,128)S(1)} fusion(f32[2,8,128,512]{3,1,2,0:T(8,128)S(1)} %pad_maximum_fusion.2, f32[1,128,2,128]{1,3,0,2:T(8,128)S(1)} %get-tuple-element.32, f32[1,128,2,128]{1,3,0,2:T(8,128)S(1)} %get-tuple-element.31), kind=kOutput, calls=%fused_computation.63 | convolution fusion | flops 3221291008 | bytes 8650752 | tf_op jit(solution)/shard_map/cbdq,ckbm->dqkm/dot_general | solution.py:77
  428.5 4.4 %copy.209 = f32[2,128,8,512]{3,2,1,0:T(8,128)} copy(f32[2,128,8,512]{3,1,2,0:T(8,128)S(1)} %fusion.41) | data formatting | bytes 8388608 | tf_op jit(solution)/shard_map/cbdq,ckbm->dqkm/dot_general | solution.py:77
  (63 shorter events, 37.7 us)
Async XLA Ops:
  12.7 12.0 %copy-start.3 = (f32[128,4096]{1,0:T(8,128)S(1)}, f32[128,4096]{1,0:T(8,128)}, u32[]{:S(2)}) copy-start(f32[128,4096]{1,0:T(8,128)} %param.4) | copy-start | bytes 6291460
  12.7 63.4 %all-to-all-start = ((f32[128,2,1,1,32,1,1,128]{7,4,1,6,5,3,2,0:T(8,128)}), f32[128,2,1,1,32,1,1,128]{7,4,1,6,5,3,2,0:T(8,128)}, u32[]{:S(2)}, u32[]{:S(2)}) async-start(f32[128,2,1,1,32,1,1,128]{7,4,1,6,5,3,2,0:T(8,128)} %bitcast.252), calls=%async_computation | async-start | bytes 8388608 | tf_op jit(solution)/shard_map/all_to_all | solution.py:29
  76.0 49.1 %all-to-all-start.2 = ((f32[128,32,128]{2,1,0:T(8,128)}), f32[128,32,128]{2,1,0:T(8,128)S(1)}, u32[]{:S(2)}, u32[]{:S(2)}) async-start(f32[128,32,128]{2,1,0:T(8,128)} %bitcast.60), calls=%async_computation.2 | async-start | bytes 4194304 | tf_op jit(solution)/shard_map/all_to_all | solution.py:142
  125.1 1.4 copy-start
  126.5 61.6 %all-to-all-start.1 = ((f32[128,2,1,1,32,1,1,128]{7,4,1,6,5,3,2,0:T(8,128)}), f32[128,2,1,1,32,1,1,128]{7,4,1,6,5,3,2,0:T(8,128)}, u32[]{:S(2)}, u32[]{:S(2)}) async-start(f32[128,2,1,1,32,1,1,128]{7,4,1,6,5,3,2,0:T(8,128)} %bitcast.253), calls=%async_computation.1 | async-start | bytes 8388608 | tf_op jit(solution)/shard_map/all_to_all | solution.py:29
  199.7 7.1 %copy-start.1 = (f32[128,32,128]{0,2,1:T(8,128)S(1)}, f32[128,32,128]{0,2,1:T(8,128)}, u32[]{:S(2)}) copy-start(f32[128,32,128]{0,2,1:T(8,128)} %get-tuple-element.25) | copy-start | bytes 6291460
  199.7 7.1 %copy-start.2 = (f32[128,32,128]{0,2,1:T(8,128)S(1)}, f32[128,32,128]{0,2,1:T(8,128)}, u32[]{:S(2)}) copy-start(f32[128,32,128]{0,2,1:T(8,128)} %get-tuple-element.26) | copy-start | bytes 6291460
  241.6 58.9 %all-to-all-start.3 = ((f32[128,2,1,1,32,1,1,128]{7,4,1,6,5,3,2,0:T(8,128)}), f32[128,2,1,1,32,1,1,128]{7,4,1,6,5,3,2,0:T(8,128)}, u32[]{:S(2)}, u32[]{:S(2)}) async-start(f32[128,2,1,1,32,1,1,128]{7,4,1,6,5,3,2,0:T(8,128)} %bitcast.255), calls=%async_computation.3 | async-start | bytes 8388608 | tf_op jit(solution)/shard_map/all_to_all | solution.py:29
  321.6 7.9 %copy-start.4 = (f32[8,1024]{1,0:T(8,128)S(1)}, f32[8,1024]{1,0:T(8,128)}, u32[]{:S(2)}) copy-start(f32[8,1024]{1,0:T(8,128)} %param.5) | copy-start | bytes 98308
  321.6 58.7 %all-to-all-start.4 = ((f32[128,2,1,1,32,1,1,128]{7,4,1,6,5,3,2,0:T(8,128)}), f32[128,2,1,1,32,1,1,128]{7,4,1,6,5,3,2,0:T(8,128)}, u32[]{:S(2)}, u32[]{:S(2)}) async-start(f32[128,2,1,1,32,1,1,128]{7,4,1,6,5,3,2,0:T(8,128)} %bitcast.254), calls=%async_computation.4 | async-start | bytes 8388608 | tf_op jit(solution)/shard_map/all_to_all | solution.py:29
  393.6 6.1 %collective-permute-start = (f32[2,7,1024]{2,1,0:T(8,128)S(1)}, f32[2,7,1024]{2,1,0:T(8,128)S(1)}, u32[]{:S(2)}, u32[]{:S(2)}) collective-permute-start(f32[2,7,1024]{2,1,0:T(8,128)S(1)} %slice.168), channel_id=1, source_target_pairs={{0,1},{1,2},{2,3},{3,4},{4,5},{5,6},{6,7},{7,8},{8,9},{9,10},{10,1... | collective-permute-start | bytes 172040 | tf_op jit(solution)/shard_map/ppermute | solution.py:37
where the time goes:
time: 441 us; the launch traced here: 433 us
  waiting for transfers between devices  191 us (43%)
  local copies, waits for them, and re-layouts  73.1 us (17%)
  matrix products  59.8 us (14%)
  other arithmetic  59.4 us (13%)
  starting transfers between devices  49.1 us (11%)
    all_to_all x4, waiting for transfers between devices, joined_exchange(): lax.all_to_all(pieces, axis, split_axis=0, concat_axis=0, tiled=True)  190 us
    sub x8, other arithmetic, complex_product(): real_part = values[0] * cos_part - values[1] * sin_part  43.3 us
    all_to_all x4, starting transfers between devices, joined_exchange(): lax.all_to_all(pieces, axis, split_axis=0, concat_axis=0, tiled=True)  37.3 us
    dot_general x3, matrix products, dft_rows(): jnp.einsum('cbdq,ckbm->dqkm', dft_table(inner_radix, direction), partial_...  17.6 us
    dot_general x3, matrix products, dft_rows(): jnp.einsum('cadk,cabm->dkbm', dft_table(outer_radix, direction), blocked,...  16.7 us
    dot_general x2, matrix products, dft_cols(): jnp.einsum('cadk,cmab->dmkb', dft_table(outer_radix, direction), blocked,...  14.4 us
    another operation x3, local copies, waits for them, and re-layouts, joined_exchange(): pieces = jnp.moveaxis(split_up(pieces, splits[1] + 1, sizes[1]), 0, 1)  13.3 us
    another operation x2, local copies, waits for them, and re-layouts, split_up(): pieces = x.reshape(*dims[:dim], size, dims[dim] // size, *dims[dim + 1:])  12.7 us
  transfers between devices with their start and end apart: 6, of which 5 were waited for; matrix products, arithmetic and copies ran while one was open for 13% of the time, Pallas kernels for 0%

commit v1 on v0

v1 whole, which is shorter than its diff:
```python
import math

import jax
import jax.numpy as jnp
import numpy as np
from jax import lax
from jax.experimental import pallas as pl
from jax.experimental.pallas import tpu as pltpu
from jax.sharding import PartitionSpec as P

DEVICES = 128
ROWS = 32
TILE = 8
PARTS = ROWS // TILE
LANES = 128
LOG_TOTAL = 26
BY_MESH = pl.DeviceIdType.MESH
F32 = jnp.float32
BF16 = jnp.bfloat16


def partner(step):
    row = lax.axis_index("row")
    col = lax.axis_index("col")
    low = lax.rem(step, 4)
    mid = low + lax.rem(step // 4, 4)
    high = mid + lax.rem(step // 16, 4)
    z = lax.rem(row // 8 + low, 4)
    y = lax.rem((col // 2) * 2 + lax.rem(row // 4, 2) + mid, 4)
    x = lax.rem(row + high, 4)
    core = lax.rem(col + step // 64, 2)
    return z * 8 + lax.rem(y, 2) * 4 + x, (y // 2) * 2 + core


def times(a, b):
    return a[0] * b[0] - a[1] * b[1], a[0] * b[1] + a[1] * b[0]


def times_conj(a, b):
    return a[0] * b[0] + a[1] * b[1], a[1] * b[0] - a[0] * b[1]


def plus(a, b):
    return a[0] + b[0], a[1] + b[1]


def minus(a, b):
    return a[0] - b[0], a[1] - b[1]


def turned(a, part, whole, sign):
    part = part % whole
    eighths = 8 * part / whole
    if eighths == 0:
        return a
    if eighths == 2:
        return (-a[1], a[0]) if sign > 0 else (a[1], -a[0])
    if eighths == 4:
        return -a[0], -a[1]
    if eighths == 6:
        return (a[1], -a[0]) if sign > 0 else (-a[1], a[0])
    angle = sign * 2.0 * math.pi * part / whole
    cos_part, sin_part = math.cos(angle), math.sin(angle)
    if eighths in (1, 3, 5, 7):
        half = math.sqrt(0.5)
        c = half if cos_part > 0 else -half
        same = (cos_part > 0) == (sin_part > 0)
        if same:
            return (a[0] - a[1]) * c, (a[0] + a[1]) * c
        return (a[0] + a[1]) * c, (a[1] - a[0]) * c
    return a[0] * cos_part - a[1] * sin_part, a[0] * sin_part + a[1] * cos_part


def small_dft(xs, sign):
    n = len(xs)
    if n == 1:
        return xs
    if n == 2:
        return [plus(xs[0], xs[1]), minus(xs[0], xs[1])]
    parts = [small_dft(xs[r::4], sign) for r in range(4)]
    out = [None] * n
    for k in range(n // 4):
        a, b, c, d = (turned(parts[r][k], r * k, n, sign) for r in range(4))
        ac, bd = plus(a, c), plus(b, d)
        ac_, bd_ = minus(a, c), turned(minus(b, d), 1, 4, sign)
        out[k] = plus(ac, bd)
        out[k + n // 4] = plus(ac_, bd_)
        out[k + n // 2] = minus(ac, bd)
        out[k + 3 * n // 4] = minus(ac_, bd_)
    return out


def block_dft(load, scratch, finish, sign):
    for low in range(8):
        values = small_dft([load(8 * high + low) for high in range(16)], sign)
        for k, value in enumerate(values):
            value = turned(value, low * k, 128, sign)
            scratch[8 * k + low, 0] = value[0]
            scratch[8 * k + low, 1] = value[1]

    def second(k, carry):
        values = small_dft(
            [(scratch[8 * k + low, 0], scratch[8 * k + low, 1]) for low in range(8)], sign
        )
        for high, value in enumerate(values):
            finish(k + 16 * high, value)
        return carry

    lax.fori_loop(0, 16, second, 0)


def quarter_sincos(angle, quarter):
    square = angle * angle
    sin_part = angle * (
        1.0 + square * (-1.0 / 6 + square * (1.0 / 120 + square * (-1.0 / 5040 + square / 362880)))
    )
    cos_part = 1.0 + square * (
        -0.5 + square * (1.0 / 24 + square * (-1.0 / 720 + square * (1.0 / 40320)))
    )
    odd = (quarter & 1) == 1
    first = jnp.where(odd, sin_part, cos_part)
    second = jnp.where(odd, cos_part, sin_part)
    return (
        jnp.where(((quarter + 1) & 2) == 2, -first, first),
        jnp.where((quarter & 2) == 2, -second, second),
    )


def unit(product, log_whole):
    quarter = (product + (1 << (log_whole - 3))) >> (log_whole - 2)
    rest = product - (quarter << (log_whole - 2))
    return quarter_sincos(rest.astype(F32) * (2.0 * math.pi / 2**log_whole), quarter)


def phase_unit(phase):
    quarter = jnp.floor(phase * (2.0 / math.pi) + 0.5)
    high = float(np.float32(1.5703125))
    angle = (phase - quarter * high) - quarter * (math.pi / 2 - high)
    return quarter_sincos(angle, quarter.astype(jnp.int32))


def halves(x):
    high = x.astype(BF16)
    return high, (x - high.astype(F32)).astype(BF16)


def kernel(
    voltage,
    phase,
    taps,
    rows_fwd,
    rows_inv,
    lanes_fwd,
    lanes_inv,
    lanes_out,
    mid_turn,
    out_turn,
    result,
    recv1,
    work,
    send2,
    recv2,
    send3,
    recv3,
    send4,
    recv4,
    phase_in,
    phase_send,
    phase_recv,
    chirp,
    table_a,
    table_b,
    tiles,
    wide,
    edge_send,
    edge_recv,
    local_sem,
    sems1,
    sems2,
    sems3,
    sems4,
    phase_sem,
    edge_sem,
    send_sems,
    out_sem,
):
    row = lax.axis_index("row")
    col = lax.axis_index("col")
    me = row * 4 + col
    sublane = lax.broadcasted_iota(jnp.int32, (ROWS, LANES), 0)
    lane = lax.broadcasted_iota(jnp.int32, (ROWS, LANES), 1)

    phase_copy = pltpu.make_async_copy(phase, phase_in, local_sem.at[0])
    phase_copy.start()
    own_copy = pltpu.make_async_copy(
        voltage.at[:, :, pl.ds(pl.multiple_of(me * LANES, LANES), LANES)],
        recv1.at[me],
        local_sem.at[1],
    )
    own_copy.start()

    barrier = pltpu.get_barrier_semaphore()

    def greet(step, carry):
        pl.semaphore_signal(barrier, inc=1, device_id=partner(step), device_id_type=BY_MESH)
        return carry

    lax.fori_loop(1, DEVICES, greet, 0)
    pl.semaphore_wait(barrier, DEVICES - 1)

    def send_piece(step, source_of, target, send_sem, recv_sem):
        to_row, to_col = partner(step)
        pltpu.make_async_remote_copy(
            src_ref=source_of(to_row * 4 + to_col),
            dst_ref=target,
            send_sem=send_sem,
            recv_sem=recv_sem,
            device_id=(to_row, to_col),
            device_id_type=BY_MESH,
        ).start()

    def tile_rows(part):
        return pl.ds(pl.multiple_of(part * TILE, TILE), TILE)

    def wait_part(buffer, sem):
        ref = buffer.at[pl.ds(0, DEVICES - 1), :, pl.ds(0, TILE), :]
        pltpu.make_async_copy(ref, ref, sem).wait()

    def voltage_part(part, carry):
        def one(step, inner):
            send_piece(
                step,
                lambda to: voltage.at[
                    :, tile_rows(part), pl.ds(pl.multiple_of(to * LANES, LANES), LANES)
                ],
                recv1.at[me, :, tile_rows(part), :],
                send_sems.at[0],
                sems1.at[part],
            )
            return inner

        lax.fori_loop(1, DEVICES, one, 0)
        return carry

    lax.fori_loop(0, PARTS, voltage_part, 0)

    phase_copy.wait()

    def phase_out(b, carry):
        block = phase_in[:, pl.ds(pl.multiple_of(b * LANES, LANES), LANES)]
        phase_send[:, pl.ds(b, 1), :] = jnp.transpose(block).reshape(DEVICES, 1, LANES)
        return carry

    lax.fori_loop(0, ROWS, phase_out, 0)

    def phase_piece(step, carry):
        send_piece(
            step, lambda to: phase_send.at[to], phase_recv.at[me], send_sems.at[1], phase_sem
        )
        return carry

    lax.fori_loop(1, DEVICES, phase_piece, 0)
    phase_recv[me] = phase_send[me]

    def fill(a, carry):
        cos_part, sin_part = unit(sublane * a, 12)
        table_a[a, 0] = cos_part
        table_a[a, 1] = -sin_part
        cos_part, sin_part = unit((a + 128 * sublane) * (128 * me + lane), LOG_TOTAL)
        table_b[a, 0] = cos_part
        table_b[a, 1] = -sin_part
        return carry

    lax.fori_loop(0, DEVICES, fill, 0)

    own_copy.wait()

    def first_part(part, carry):
        wait_part(recv1, sems1.at[part])
        at = tile_rows(part)

        def load(n):
            return recv1[n, 0, at, :], recv1[n, 1, at, :]

        def finish(k, value):
            turn = table_a[k, 0, at, :], table_a[k, 1, at, :]
            value = times(value, turn)
            work[k, 0, at, :] = value[0]
            work[k, 1, at, :] = value[1]

        block_dft(load, tiles, finish, -1)
        return carry

    lax.fori_loop(0, PARTS, first_part, 0)

    def row_dft(matrix, first, second):
        high, low = halves(
            jnp.concatenate([first.reshape(64, LANES), second.reshape(64, LANES)], axis=1)
        )
        return jnp.dot(
            matrix[...],
            jnp.concatenate([high, low, high], axis=0),
            preferred_element_type=F32,
        )

    def index_of(step):
        to_row, to_col = partner(step)
        return to_row * 4 + to_col

    def second_step(pair, carry):
        places = index_of(2 * pair), index_of(2 * pair + 1)
        both = row_dft(rows_fwd, work[places[0]], work[places[1]])
        for at, place in enumerate(places):
            value = (
                both[:ROWS, at * LANES : (at + 1) * LANES],
                both[ROWS:, at * LANES : (at + 1) * LANES],
            )
            value = times(value, (table_b[place, 0], table_b[place, 1]))
            send2[place, 0] = value[0]
            send2[place, 1] = value[1]
        return carry

    def send_part(buffer, target, part, send_sem, recv_sem):
        def one(step, inner):
            send_piece(
                step,
                lambda to: buffer.at[to, :, tile_rows(part), :],
                target.at[me, :, tile_rows(part), :],
                send_sem,
                recv_sem,
            )
            return inner

        lax.fori_loop(1, DEVICES, one, 0)

    lax.fori_loop(0, DEVICES // 2, second_step, 0)
    recv2[me] = send2[me]

    def send2_part(part, carry):
        send_part(send2, recv2, part, send_sems.at[2], sems2.at[part])
        return carry

    lax.fori_loop(0, PARTS, send2_part, 0)

    phase_all = phase_recv.at[pl.ds(0, DEVICES - 1)]
    pltpu.make_async_copy(phase_all, phase_all, phase_sem).wait()

    def phase_back(b, carry):
        block = phase_recv[:, pl.ds(b, 1), :].reshape(DEVICES, LANES)
        cos_part, sin_part = phase_unit(jnp.transpose(block))
        chirp[:, 0, pl.ds(b, 1), :] = cos_part.reshape(DEVICES, 1, LANES)
        chirp[:, 1, pl.ds(b, 1), :] = sin_part.reshape(DEVICES, 1, LANES)
        return carry

    lax.fori_loop(0, ROWS, phase_back, 0)

    def refill(h, carry):
        cos_part, sin_part = unit((me + 128 * sublane) * (128 * h + lane), LOG_TOTAL)
        table_b[h, 0] = cos_part
        table_b[h, 1] = sin_part
        return carry

    lax.fori_loop(0, DEVICES, refill, 0)

    def middle_part(part, carry):
        wait_part(recv2, sems2.at[part])
        at = tile_rows(part)

        def load(n):
            return recv2[n, 0, at, :], recv2[n, 1, at, :]

        def finish(k, value):
            turn = mid_turn[0, pl.ds(k, 1), :], mid_turn[1, pl.ds(k, 1), :]
            value = times(value, turn)
            wide[k, :, :LANES] = value[0]
            wide[k, :, LANES:] = value[1]

        block_dft(load, tiles, finish, -1)

        def lanes_step(group, inner):
            rows = pl.ds(group * 32, 32)
            high, low = halves(wide[rows].reshape(32 * TILE, 2 * LANES))
            there = jnp.dot(
                jnp.concatenate([high, low, high], axis=1),
                lanes_fwd[...],
                preferred_element_type=F32,
            )
            turn = (
                chirp[rows, 0, at, :].reshape(32 * TILE, LANES),
                chirp[rows, 1, at, :].reshape(32 * TILE, LANES),
            )
            there = times((there[:, :LANES], there[:, LANES:]), turn)
            high, low = halves(jnp.concatenate(there, axis=1))
            back = jnp.dot(
                jnp.concatenate([high, low, high], axis=1),
                lanes_inv[...],
                preferred_element_type=F32,
            )
            wide[rows] = back.reshape(32, TILE, 2 * LANES)
            return inner

        lax.fori_loop(0, 4, lanes_step, 0)

        def load_back(n):
            turn = mid_turn[0, pl.ds(n, 1), :], mid_turn[1, pl.ds(n, 1), :]
            return times_conj((wide[n, :, :LANES], wide[n, :, LANES:]), turn)

        def finish_back(k, value):
            value = times(value, (table_b[k, 0, at, :], table_b[k, 1, at, :]))
            send3[k, 0, at, :] = value[0]
            send3[k, 1, at, :] = value[1]

        block_dft(load_back, tiles, finish_back, 1)
        recv3[me, :, at, :] = send3[me, :, at, :]
        send_part(send3, recv3, part, send_sems.at[3], sems3.at[part])
        return carry

    lax.fori_loop(0, PARTS, middle_part, 0)

    def wait3(part, carry):
        wait_part(recv3, sems3.at[part])
        return carry

    lax.fori_loop(0, PARTS, wait3, 0)

    def third_step(pair, carry):
        both = row_dft(rows_inv, recv3[2 * pair], recv3[2 * pair + 1])
        for at in range(2):
            place = 2 * pair + at
            value = (
                both[:ROWS, at * LANES : (at + 1) * LANES],
                both[ROWS:, at * LANES : (at + 1) * LANES],
            )
            value = times_conj(value, (table_a[place, 0], table_a[place, 1]))
            work[place, 0] = value[0]
            work[place, 1] = value[1]
        return carry

    lax.fori_loop(0, DEVICES // 2, third_step, 0)

    def fourth_part(turn, carry):
        part = PARTS - 1 - turn
        at = tile_rows(part)

        def load(n):
            return work[n, 0, at, :], work[n, 1, at, :]

        def finish(k, value):
            send4[k, 0, at, :] = value[0]
            send4[k, 1, at, :] = value[1]

        block_dft(load, tiles, finish, 1)
        recv4[me, :, at, :] = send4[me, :, at, :]
        send_part(send4, recv4, part, send_sems.at[4], sems4.at[part])
        return carry

    lax.fori_loop(0, PARTS, fourth_part, 0)

    wait_part(recv4, sems4.at[3])

    def edge_out(j, carry):
        edge_send[j, 0:1, :] = recv4[72 + j, 0, ROWS - 1 : ROWS, :]
        edge_send[j, 1:2, :] = recv4[72 + j, 1, ROWS - 1 : ROWS, :]
        return carry

    lax.fori_loop(0, 56, edge_out, 0)
    following = lax.rem(me + 1, DEVICES)
    edge_copy = pltpu.make_async_remote_copy(
        src_ref=edge_send,
        dst_ref=edge_recv,
        send_sem=send_sems.at[5],
        recv_sem=edge_sem,
        device_id=(following // 4, lax.rem(following, 4)),
        device_id_type=BY_MESH,
    )
    edge_copy.start()
    first_row = lax.broadcasted_iota(jnp.int32, (TILE, LANES), 0) == 0
    ahead = me > 0

    def filter_half(half):
        tile_list = (2 * half, 2 * half + 1)

        def one_position(high, carry):
            weights = [
                taps[t : t + 1, pl.ds(pl.multiple_of(high * LANES, LANES), LANES)]
                for t in range(8)
            ]
            for part in tile_list:
                at = slice(part * TILE, part * TILE + TILE)
                for c in range(2):
                    now = [recv4[8 * m + high, c, at, :] for m in range(16)]
                    old = [None] * 16
                    for m in range(9, 16):
                        shifted = pltpu.roll(now[m], 1, 0)
                        if part == 0:
                            edge = edge_recv[8 * (m - 9) + high, c : c + 1, :]
                            edge = jnp.where(ahead, edge, 0.0)
                        else:
                            edge = recv4[8 * m + high, c, part * TILE - 1 : part * TILE, :]
                        old[m] = jnp.where(first_row, edge, shifted)
                    for m in range(16):
                        total = weights[0] * now[m]
                        for t in range(1, 8):
                            total = total + weights[t] * (now[m - t] if m >= t else old[m - t + 16])
                        work[16 * high + m, c, at, :] = total
            return carry

        lax.fori_loop(0, 8, one_position, 0)

        def one_frame(m, carry):
            for at_tile, part in enumerate(tile_list):
                at = slice(part * TILE, part * TILE + TILE)
                values = small_dft(
                    [(work[16 * high + m, 0, at, :], work[16 * high + m, 1, at, :]) for high in range(8)],
                    -1,
                )
                for a, value in enumerate(values):
                    value = times(value, (out_turn[0, a : a + 1, :], out_turn[1, a : a + 1, :]))
                    for c in range(2):
                        tiles_out[a, c, pl.ds(128 * at_tile + m, TILE, stride=16), :] = value[c]
            return carry

        lax.fori_loop(0, 16, one_frame, 0)

        def one_class(a, carry):
            frames = jnp.concatenate([tiles_out[a, 0], tiles_out[a, 1]], axis=1)
            high, low = halves(frames)
            both = lax.dot_general(
                lanes_out[...],
                jnp.concatenate([high, low, high], axis=1),
                (((1,), (1,)), ((), ())),
                preferred_element_type=F32,
            )
            for c in range(2):
                for side in range(2):
                    gathered[c, 2 * half + side, pl.ds(a, 128, stride=8), :] = both[
                        c * 128 : c * 128 + 128, side * LANES : side * LANES + LANES
                    ]
            return carry

        lax.fori_loop(0, 8, one_class, 0)
        for side in range(2):
            column = 2 * half + side
            pltpu.make_async_copy(
                gathered.at[:, column],
                result.at[:, :, pl.ds(column * LANES, LANES)],
                out_sem.at[column],
            ).start()

    tiles_out = table_a.reshape(16, 2, 256, LANES)
    gathered = table_b.reshape(2, 4, 1024, LANES)

    wait_part(recv4, sems4.at[2])
    wait_part(recv4, sems4.at[1])
    filter_half(1)
    wait_part(recv4, sems4.at[0])
    edge_copy.wait_recv()
    filter_half(0)

    for column in range(4):
        pltpu.make_async_copy(
            gathered.at[:, column],
            result.at[:, :, pl.ds(column * LANES, LANES)],
            out_sem.at[column],
        ).wait()
    edge_copy.wait_send()
    pieces = recv1.at[pl.ds(0, DEVICES - 1)]
    for at in (0, 2, 3, 4):
        pltpu.make_async_copy(pieces, pieces, send_sems.at[at]).wait()
    pltpu.make_async_copy(phase_all, phase_all, send_sems.at[1]).wait()


def dft_parts(size, sign, scale=1.0):
    digits = np.arange(size)
    angle = sign * 2.0 * np.pi * ((digits[:, None] * digits[None, :]) % size) / size
    return scale * np.cos(angle), scale * np.sin(angle)


def bf16_halves(matrix):
    matrix = np.asarray(matrix, np.float32)
    high = matrix.astype(BF16)
    return high, (matrix - high.astype(np.float32)).astype(BF16)


def left_matrix(size, sign):
    c, s = dft_parts(size, sign)
    high, low = bf16_halves(np.block([[c, -s], [s, c]]))
    return np.concatenate([high, high, low], axis=1)


def right_matrix(size, sign, scale=1.0):
    c, s = dft_parts(size, sign, scale)
    high, low = bf16_halves(np.block([[c, s], [-s, c]]))
    return np.concatenate([high, high, low], axis=0)


def turn_table(rows, cols, whole):
    product = np.arange(rows)[:, None] * np.arange(cols)[None, :] % whole
    angle = -2.0 * np.pi * product / whole
    return np.stack([np.cos(angle), np.sin(angle)]).astype(np.float32)


def local(voltage, chirp_phase, filter_taps):
    constants = [
        left_matrix(ROWS, -1),
        left_matrix(ROWS, 1),
        right_matrix(LANES, -1),
        right_matrix(LANES, 1, 2.0**-LOG_TOTAL),
        left_matrix(LANES, -1),
        turn_table(128, LANES, 128 * LANES),
        turn_table(8, LANES, 8 * LANES),
    ]
    blocks = pltpu.VMEM((DEVICES, 2, ROWS, LANES), F32)
    phases = pltpu.VMEM((DEVICES, ROWS, LANES), F32)
    in_vmem = pl.BlockSpec(memory_space=pltpu.VMEM)
    in_hbm = pl.BlockSpec(memory_space=pl.ANY)
    return pl.pallas_call(
        kernel,
        out_shape=jax.ShapeDtypeStruct((2, 1024, 512), F32),
        in_specs=[in_hbm, in_hbm] + [in_vmem] * (1 + len(constants)),
        out_specs=in_hbm,
        scratch_shapes=[blocks] * 8
        + [pltpu.VMEM((DEVICES, 4096), F32)]
        + [phases] * 2
        + [blocks] * 3
        + [
            pltpu.VMEM((DEVICES, 2, TILE, LANES), F32),
            pltpu.VMEM((DEVICES, TILE, 2 * LANES), F32),
            pltpu.VMEM((56, 2, LANES), F32),
            pltpu.VMEM((56, 2, LANES), F32),
            pltpu.SemaphoreType.DMA((2,)),
            pltpu.SemaphoreType.DMA((PARTS,)),
            pltpu.SemaphoreType.DMA((PARTS,)),
            pltpu.SemaphoreType.DMA((PARTS,)),
            pltpu.SemaphoreType.DMA((PARTS,)),
            pltpu.SemaphoreType.DMA,
            pltpu.SemaphoreType.DMA,
            pltpu.SemaphoreType.DMA((6,)),
            pltpu.SemaphoreType.DMA((4,)),
        ],
        compiler_params=pltpu.CompilerParams(
            collective_id=0, has_side_effects=True, vmem_limit_bytes=67043328
        ),
    )(voltage, chirp_phase, filter_taps, *[jnp.asarray(c) for c in constants])


def solution(mesh):
    in_specs = (P(None, ("row", "col"), None), P(("row", "col"), None), P())
    out_specs = P(None, None, ("row", "col"))
    return jax.shard_map(local, mesh=mesh, in_specs=in_specs, out_specs=out_specs, check_vma=False)
```

time: 441 us -> 251 us (0.57); the launches traced: 433 us -> 251 us
  Pallas kernels: 0 us -> 246 us
  waiting for transfers between devices: 191 us -> 0 us
  local copies, waits for them, and re-layouts: 73.1 us -> 4.64 us
  matrix products: 59.8 us -> 0 us
  other arithmetic: 59.4 us -> 0 us
  starting transfers between devices: 49.1 us -> 0 us
    pallas_call x0 -> x1, Pallas kernels: none -> 246 us  [local(): pl.pallas_call(kernel, out_shape=jax.ShapeDtypeStruct((2, 1024, 512), F32...]
    all_to_all x5 -> x0, waiting for transfers between devices: 190 us -> none  [the longest x4 190 us: joined_exchange(): lax.all_to_all(pieces, axis, split_axis=0, concat_axis=0, tiled=True)]
    dot_general x10 -> x0, matrix products: 59.8 us -> none  [the longest x3 17.6 us: dft_rows(): jnp.einsum('cbdq,ckbm->dqkm', dft_table(inner_radix, direction), partial_...]
    all_to_all x5 -> x0, starting transfers between devices: 44.2 us -> none  [the longest x4 37.3 us: joined_exchange(): lax.all_to_all(pieces, axis, split_axis=0, concat_axis=0, tiled=True)]
    sub x8 -> x0, other arithmetic: 43.3 us -> none  [complex_product(): real_part = values[0] * cos_part - values[1] * sin_part]
    another operation x8 -> x0, local copies, waits for them, and re-layouts: 31.6 us -> none  [the longest x3 13.3 us: joined_exchange(): pieces = jnp.moveaxis(split_up(pieces, splits[1] + 1, sizes[1]), 0, 1)]
    transpose x2 -> x0, local copies, waits for them, and re-layouts: 9.23 us -> none  [laid_out(): pieces = jnp.moveaxis(pieces, 0, dim)]
    sin x2 -> x0, local copies, waits for them, and re-layouts: 8.33 us -> none  [the longest x1 8.23 us: local(): signal = complex_product(signal, jnp.cos(local_phase), jnp.sin(local_phase))]
  transfers between devices with their start and end apart: 6 -> 0, of which waited for: 5 -> 0; matrix products, arithmetic and copies ran while one was open for 13% -> 0% of each run, Pallas kernels for 0% -> 0%
where the time goes in v1:
time: 251 us
  Pallas kernels  246 us (98%)
  local copies, waits for them, and re-layouts  4.64 us (2%)
    pallas_call x1, Pallas kernels, local(): pl.pallas_call(kernel, out_shape=jax.ShapeDtypeStruct((2, 1024, 512), F32...  246 us

profile of v1, /device:TPU:1, one launch (start us, length us, event | category | flops | bytes accessed | tf_op | source)
XLA Modules:
  0.0 250.7 jit_solution(364246432675829233)
XLA Ops:
  0.0 246.1 %shard_map.100 = f32[2,1024,512]{2,1,0:T(8,128)} custom-call(f32[2,32,16384]{2,1,0:T(8,128)} %voltage.1, f32[128,4096]{1,0:T(8,128)} %phase.1, f32[8,1024]{1,0:T(8,128)} %taps.1, bf16[64,192]{1,0:T(8,128)(2,1)} %constant.14.clone.rows_fwd, bf16[64,192]{1,0:T(8,128)(2,1)} %constant.15.clone.rows_inv, bf16[768,256]{1,0:T(8,128)(2,1)} %constant.16.clone.lanes_fwd, ...), custom_call_target="tpu_custom_call" | custom-call | tf_op jit(solution)/shard_map/pallas_call | solution.py:617
  246.1 4.6 %copy.12 = f32[2,1024,512]{2,1,0:T(8,128)} copy(f32[2,1024,512]{2,1,0:T(8,128)} %shard_map.100) | data formatting | bytes 8388608

commit v2 on v1

--- a/solution.py
+++ b/solution.py
@@ -14,22 +14,28 @@
 PARTS = ROWS // TILE
 LANES = 128
 LOG_TOTAL = 26
+GROUPS = DEVICES // 16
+CONSTANTS = 8
 BY_MESH = pl.DeviceIdType.MESH
 F32 = jnp.float32
 BF16 = jnp.bfloat16
 
 
-def partner(step):
-    row = lax.axis_index("row")
-    col = lax.axis_index("col")
+def device_at(z, y, x, core):
+    return z * 8 + lax.rem(y, 2) * 4 + x, (y // 2) * 2 + core
+
+
+def partner(here, step, way=1):
+    z, y, x, core = here
     low = lax.rem(step, 4)
     mid = low + lax.rem(step // 4, 4)
     high = mid + lax.rem(step // 16, 4)
-    z = lax.rem(row // 8 + low, 4)
-    y = lax.rem((col // 2) * 2 + lax.rem(row // 4, 2) + mid, 4)
-    x = lax.rem(row + high, 4)
-    core = lax.rem(col + step // 64, 2)
-    return z * 8 + lax.rem(y, 2) * 4 + x, (y // 2) * 2 + core
+    return device_at(
+        lax.rem(z + way * low, 4),
+        lax.rem(y + way * mid, 4),
+        lax.rem(x + way * high, 4),
+        lax.rem(core + step // 64, 2),
+    )
 
 
 def times(a, b):
@@ -144,18 +150,26 @@
     return high, (x - high.astype(F32)).astype(BF16)
 
 
+def frames_dft(matrix, real_part, imag_part):
+    high, low = halves(jnp.concatenate([real_part, imag_part], axis=1))
+    return lax.dot_general(
+        matrix[...],
+        jnp.concatenate([high, low, high], axis=1),
+        (((1,), (1,)), ((), ())),
+        preferred_element_type=F32,
+    )
+
+
 def kernel(
     voltage,
     phase,
-    taps,
-    rows_fwd,
-    rows_inv,
-    lanes_fwd,
-    lanes_inv,
-    lanes_out,
-    mid_turn,
-    out_turn,
-    result,
+    *refs,
+):
+    given, refs = refs[:CONSTANTS], refs[CONSTANTS:]
+    late, ready, refs = refs[0], refs[1], refs[2:]
+    held, refs = refs[:CONSTANTS], refs[CONSTANTS:]
+    taps, rows_fwd, rows_inv, lanes_fwd, lanes_inv, lanes_out, mid_turn, out_turn = held
+    (
     recv1,
     work,
     send2,
@@ -183,7 +197,9 @@
     edge_sem,
     send_sems,
     out_sem,
-):
+    given_sem,
+    plane_sem,
+    ) = refs
     row = lax.axis_index("row")
     col = lax.axis_index("col")
     me = row * 4 + col
@@ -198,18 +214,40 @@
         local_sem.at[1],
     )
     own_copy.start()
-
+    given_copies = [
+        pltpu.make_async_copy(a, b, given_sem.at[n]) for n, (a, b) in enumerate(zip(given, held))
+    ]
+    for copy in given_copies:
+        copy.start()
+
+    place = row // 8, (col // 2) * 2 + lax.rem(row // 4, 2), lax.rem(row, 4), lax.rem(col, 2)
+    z, y, x, core = place
     barrier = pltpu.get_barrier_semaphore()
 
     def greet(step, carry):
-        pl.semaphore_signal(barrier, inc=1, device_id=partner(step), device_id_type=BY_MESH)
-        return carry
-
-    lax.fori_loop(1, DEVICES, greet, 0)
-    pl.semaphore_wait(barrier, DEVICES - 1)
+        to = device_at(
+            z,
+            lax.rem(y + lax.rem(step, 4), 4),
+            lax.rem(x + lax.rem(step // 4, 4), 4),
+            lax.rem(core + step // 16, 2),
+        )
+        pl.semaphore_signal(barrier, inc=1, device_id=to, device_id_type=BY_MESH)
+        return carry
+
+    def greet_along(other):
+        to = device_at(lax.rem(z + other, 4), y, x, core)
+        return dict(inc=1, device_id=to, device_id_type=BY_MESH)
+
+    for other in range(1, 4):
+        pl.semaphore_signal(barrier, **greet_along(other))
+    lax.fori_loop(1, 32, greet, 0)
+    pl.semaphore_wait(barrier, 34)
+    for other in range(1, 4):
+        pl.semaphore_signal(plane_sem, **greet_along(other))
+    pl.semaphore_wait(plane_sem, 3)
 
     def send_piece(step, source_of, target, send_sem, recv_sem):
-        to_row, to_col = partner(step)
+        to_row, to_col = partner(place, step)
         pltpu.make_async_remote_copy(
             src_ref=source_of(to_row * 4 + to_col),
             dst_ref=target,
@@ -293,6 +331,9 @@
 
     lax.fori_loop(0, PARTS, first_part, 0)
 
+    for copy in given_copies:
+        copy.wait()
+
     def row_dft(matrix, first, second):
         high, low = halves(
             jnp.concatenate([first.reshape(64, LANES), second.reshape(64, LANES)], axis=1)
@@ -303,41 +344,39 @@
             preferred_element_type=F32,
         )
 
-    def index_of(step):
-        to_row, to_col = partner(step)
-        return to_row * 4 + to_col
-
-    def second_step(pair, carry):
-        places = index_of(2 * pair), index_of(2 * pair + 1)
-        both = row_dft(rows_fwd, work[places[0]], work[places[1]])
-        for at, place in enumerate(places):
-            value = (
-                both[:ROWS, at * LANES : (at + 1) * LANES],
-                both[ROWS:, at * LANES : (at + 1) * LANES],
-            )
-            value = times(value, (table_b[place, 0], table_b[place, 1]))
-            send2[place, 0] = value[0]
-            send2[place, 1] = value[1]
-        return carry
-
-    def send_part(buffer, target, part, send_sem, recv_sem):
+    def row_dfts(matrix, source, places):
+        done = []
+        for first, second in zip(places[::2], places[1::2]):
+            both = row_dft(matrix, source[first], source[second])
+            done.append((first, (both[:ROWS, :LANES], both[ROWS:, :LANES])))
+            done.append((second, (both[:ROWS, LANES:], both[ROWS:, LANES:])))
+        return done
+
+    def second_step(group, carry):
+        for at, value in row_dfts(rows_fwd, work, [8 * group + n for n in range(8)]):
+            value = times(value, (table_b[at, 0], table_b[at, 1]))
+            send2[at, 0] = value[0]
+            send2[at, 1] = value[1]
+        return carry
+
+    def send_part(buffer, target, part, send_sem, recv_sem_of):
         def one(step, inner):
             send_piece(
                 step,
                 lambda to: buffer.at[to, :, tile_rows(part), :],
                 target.at[me, :, tile_rows(part), :],
                 send_sem,
-                recv_sem,
+                recv_sem_of(step),
             )
             return inner
 
         lax.fori_loop(1, DEVICES, one, 0)
 
-    lax.fori_loop(0, DEVICES // 2, second_step, 0)
+    lax.fori_loop(0, DEVICES // 8, second_step, 0)
     recv2[me] = send2[me]
 
     def send2_part(part, carry):
-        send_part(send2, recv2, part, send_sems.at[2], sems2.at[part])
+        send_part(send2, recv2, part, send_sems.at[2], lambda step: sems2.at[part])
         return carry
 
     lax.fori_loop(0, PARTS, send2_part, 0)
@@ -412,31 +451,43 @@
 
         block_dft(load_back, tiles, finish_back, 1)
         recv3[me, :, at, :] = send3[me, :, at, :]
-        send_part(send3, recv3, part, send_sems.at[3], sems3.at[part])
+        send_part(
+            send3, recv3, part, send_sems.at[3], lambda step: sems3.at[GROUPS * part + step // 16]
+        )
         return carry
 
     lax.fori_loop(0, PARTS, middle_part, 0)
 
-    def wait3(part, carry):
-        wait_part(recv3, sems3.at[part])
-        return carry
-
-    lax.fori_loop(0, PARTS, wait3, 0)
-
-    def third_step(pair, carry):
-        both = row_dft(rows_inv, recv3[2 * pair], recv3[2 * pair + 1])
-        for at in range(2):
-            place = 2 * pair + at
-            value = (
-                both[:ROWS, at * LANES : (at + 1) * LANES],
-                both[ROWS:, at * LANES : (at + 1) * LANES],
-            )
-            value = times_conj(value, (table_a[place, 0], table_a[place, 1]))
-            work[place, 0] = value[0]
-            work[place, 1] = value[1]
-        return carry
-
-    lax.fori_loop(0, DEVICES // 2, third_step, 0)
+    def third_step(group, half):
+        places = []
+        for n in range(8):
+            from_row, from_col = partner(place, 16 * group + 8 * half + n, 3)
+            places.append(from_row * 4 + from_col)
+        for at, value in row_dfts(rows_inv, recv3, places):
+            value = times_conj(value, (table_a[at, 0], table_a[at, 1]))
+            work[at, 0] = value[0]
+            work[at, 1] = value[1]
+
+    def third_group(group, count):
+        def wait_one(part, inner):
+            ref = recv3.at[pl.ds(0, count), :, pl.ds(0, TILE), :]
+            pltpu.make_async_copy(ref, ref, sems3.at[GROUPS * part + group]).wait()
+            return inner
+
+        lax.fori_loop(0, PARTS, wait_one, 0)
+
+        def one(half, inner):
+            third_step(group, half)
+            return inner
+
+        lax.fori_loop(0, 2, one, 0)
+
+    def later_group(group, carry):
+        third_group(group, 16)
+        return carry
+
+    third_group(0, 15)
+    lax.fori_loop(1, GROUPS, later_group, 0)
 
     def fourth_part(turn, carry):
         part = PARTS - 1 - turn
@@ -451,7 +502,7 @@
 
         block_dft(load, tiles, finish, 1)
         recv4[me, :, at, :] = send4[me, :, at, :]
-        send_part(send4, recv4, part, send_sems.at[4], sems4.at[part])
+        send_part(send4, recv4, part, send_sems.at[4], lambda step: sems4.at[part])
         return carry
 
     lax.fori_loop(0, PARTS, fourth_part, 0)
@@ -478,37 +529,45 @@
     ahead = me > 0
 
     def filter_half(half):
-        tile_list = (2 * half, 2 * half + 1)
-
-        def one_position(high, carry):
+        tile_list = (2 * half + 1, 2 * half)
+        tiles_out = all_tiles.at[half]
+
+        def one_position(high, part):
             weights = [
                 taps[t : t + 1, pl.ds(pl.multiple_of(high * LANES, LANES), LANES)]
                 for t in range(8)
             ]
+            at = slice(part * TILE, part * TILE + TILE)
+            for c in range(2):
+                now = [recv4[8 * m + high, c, at, :] for m in range(16)]
+                old = [None] * 16
+                for m in range(9, 16):
+                    shifted = pltpu.roll(now[m], 1, 0)
+                    if part == 0:
+                        edge = edge_recv[8 * (m - 9) + high, c : c + 1, :]
+                        edge = jnp.where(ahead, edge, 0.0)
+                    else:
+                        edge = recv4[8 * m + high, c, part * TILE - 1 : part * TILE, :]
+                    old[m] = jnp.where(first_row, edge, shifted)
+                for m in range(16):
+                    total = weights[0] * now[m]
+                    for t in range(1, 8):
+                        total = total + weights[t] * (now[m - t] if m >= t else old[m - t + 16])
+                    work[16 * high + m, c, at, :] = total
+
+        for part in tile_list:
+            if part == 0:
+                edge_copy.wait_recv()
+
+            def position_of(high, carry, part=part):
+                one_position(high, part)
+                return carry
+
+            lax.fori_loop(0, 8, position_of, 0)
+
+        def one_frame(m, carry):
             for part in tile_list:
-                at = slice(part * TILE, part * TILE + TILE)
-                for c in range(2):
-                    now = [recv4[8 * m + high, c, at, :] for m in range(16)]
-                    old = [None] * 16
-                    for m in range(9, 16):
-                        shifted = pltpu.roll(now[m], 1, 0)
-                        if part == 0:
-                            edge = edge_recv[8 * (m - 9) + high, c : c + 1, :]
-                            edge = jnp.where(ahead, edge, 0.0)
-                        else:
-                            edge = recv4[8 * m + high, c, part * TILE - 1 : part * TILE, :]
-                        old[m] = jnp.where(first_row, edge, shifted)
-                    for m in range(16):
-                        total = weights[0] * now[m]
-                        for t in range(1, 8):
-                            total = total + weights[t] * (now[m - t] if m >= t else old[m - t + 16])
-                        work[16 * high + m, c, at, :] = total
-            return carry
-
-        lax.fori_loop(0, 8, one_position, 0)
-
-        def one_frame(m, carry):
-            for at_tile, part in enumerate(tile_list):
+                at_tile = part % 2
                 at = slice(part * TILE, part * TILE + TILE)
                 values = small_dft(
                     [(work[16 * high + m, 0, at, :], work[16 * high + m, 1, at, :]) for high in range(8)],
@@ -522,52 +581,75 @@
 
         lax.fori_loop(0, 16, one_frame, 0)
 
+        if half == 0:
+            return
+
         def one_class(a, carry):
-            frames = jnp.concatenate([tiles_out[a, 0], tiles_out[a, 1]], axis=1)
-            high, low = halves(frames)
-            both = lax.dot_general(
-                lanes_out[...],
-                jnp.concatenate([high, low, high], axis=1),
-                (((1,), (1,)), ((), ())),
-                preferred_element_type=F32,
-            )
+            both = frames_dft(lanes_out, tiles_out[a, 0], tiles_out[a, 1])
             for c in range(2):
                 for side in range(2):
-                    gathered[c, 2 * half + side, pl.ds(a, 128, stride=8), :] = both[
+                    gathered[side, c, pl.ds(a, 128, stride=8), :] = both[
                         c * 128 : c * 128 + 128, side * LANES : side * LANES + LANES
                     ]
             return carry
 
         lax.fori_loop(0, 8, one_class, 0)
-        for side in range(2):
-            column = 2 * half + side
-            pltpu.make_async_copy(
-                gathered.at[:, column],
-                result.at[:, :, pl.ds(column * LANES, LANES)],
-                out_sem.at[column],
-            ).start()
-
-    tiles_out = table_a.reshape(16, 2, 256, LANES)
-    gathered = table_b.reshape(2, 4, 1024, LANES)
+        ready_copy.start()
+
+    all_tiles = table_a.reshape(2, 8, 2, 256, LANES)
+    gathered = table_b.reshape(4, 2, 1024, LANES).at[pl.ds(0, 2)]
+    ready_copy = pltpu.make_async_copy(gathered, ready, out_sem.at[0])
+    late_copy = pltpu.make_async_copy(all_tiles.at[0], late, out_sem.at[1])
 
     wait_part(recv4, sems4.at[2])
     wait_part(recv4, sems4.at[1])
     filter_half(1)
     wait_part(recv4, sems4.at[0])
-    edge_copy.wait_recv()
     filter_half(0)
 
-    for column in range(4):
-        pltpu.make_async_copy(
-            gathered.at[:, column],
-            result.at[:, :, pl.ds(column * LANES, LANES)],
-            out_sem.at[column],
-        ).wait()
+    late_copy.start()
+    ready_copy.wait()
+    late_copy.wait()
     edge_copy.wait_send()
     pieces = recv1.at[pl.ds(0, DEVICES - 1)]
     for at in (0, 2, 3, 4):
         pltpu.make_async_copy(pieces, pieces, send_sems.at[at]).wait()
     pltpu.make_async_copy(phase_all, phase_all, send_sems.at[1]).wait()
+
+
+def last_kernel(late, ready, lanes_out, result, frames, passing, gathered, matrix, sems, more):
+    frame_copies = [pltpu.make_async_copy(late.at[a], frames.at[a], sems.at[a]) for a in range(8)]
+    matrix_copy = pltpu.make_async_copy(lanes_out, matrix, more.at[0])
+    pass_in = pltpu.make_async_copy(ready, passing, more.at[1])
+
+    def to_result(source, side, column, sem):
+        return pltpu.make_async_copy(
+            source.at[side], result.at[:, :, pl.ds(column * LANES, LANES)], sem
+        )
+
+    passed = [to_result(passing, side, 2 + side, more.at[2 + side]) for side in range(2)]
+    computed = [to_result(gathered, side, side, more.at[4 + side]) for side in range(2)]
+    matrix_copy.start()
+    for copy in frame_copies:
+        copy.start()
+    pass_in.start()
+    matrix_copy.wait()
+    for a in range(8):
+        frame_copies[a].wait()
+        both = frames_dft(matrix, frames[a, 0], frames[a, 1])
+        for c in range(2):
+            for side in range(2):
+                gathered[side, c, pl.ds(a, 128, stride=8), :] = both[
+                    c * 128 : c * 128 + 128, side * LANES : side * LANES + LANES
+                ]
+        if a == 3:
+            pass_in.wait()
+            for copy in passed:
+                copy.start()
+    for copy in computed:
+        copy.start()
+    for copy in passed + computed:
+        copy.wait()
 
 
 def dft_parts(size, sign, scale=1.0):
@@ -612,14 +694,18 @@
     ]
     blocks = pltpu.VMEM((DEVICES, 2, ROWS, LANES), F32)
     phases = pltpu.VMEM((DEVICES, ROWS, LANES), F32)
-    in_vmem = pl.BlockSpec(memory_space=pltpu.VMEM)
     in_hbm = pl.BlockSpec(memory_space=pl.ANY)
-    return pl.pallas_call(
+    given = [filter_taps] + [jnp.asarray(c) for c in constants]
+    late, ready = pl.pallas_call(
         kernel,
-        out_shape=jax.ShapeDtypeStruct((2, 1024, 512), F32),
-        in_specs=[in_hbm, in_hbm] + [in_vmem] * (1 + len(constants)),
-        out_specs=in_hbm,
-        scratch_shapes=[blocks] * 8
+        out_shape=[
+            jax.ShapeDtypeStruct((8, 2, 256, LANES), F32),
+            jax.ShapeDtypeStruct((2, 2, 1024, LANES), F32),
+        ],
+        in_specs=[in_hbm] * (2 + len(given)),
+        out_specs=[in_hbm] * 2,
+        scratch_shapes=[pltpu.VMEM(c.shape, c.dtype) for c in given]
+        + [blocks] * 8
         + [pltpu.VMEM((DEVICES, 4096), F32)]
         + [phases] * 2
         + [blocks] * 3
@@ -631,17 +717,34 @@
             pltpu.SemaphoreType.DMA((2,)),
             pltpu.SemaphoreType.DMA((PARTS,)),
             pltpu.SemaphoreType.DMA((PARTS,)),
-            pltpu.SemaphoreType.DMA((PARTS,)),
+            pltpu.SemaphoreType.DMA((PARTS * GROUPS,)),
             pltpu.SemaphoreType.DMA((PARTS,)),
             pltpu.SemaphoreType.DMA,
             pltpu.SemaphoreType.DMA,
             pltpu.SemaphoreType.DMA((6,)),
-            pltpu.SemaphoreType.DMA((4,)),
+            pltpu.SemaphoreType.DMA((2,)),
+            pltpu.SemaphoreType.DMA((CONSTANTS,)),
+            pltpu.SemaphoreType.REGULAR,
         ],
         compiler_params=pltpu.CompilerParams(
             collective_id=0, has_side_effects=True, vmem_limit_bytes=67043328
         ),
-    )(voltage, chirp_phase, filter_taps, *[jnp.asarray(c) for c in constants])
+    )(voltage, chirp_phase, *given)
+    return pl.pallas_call(
+        last_kernel,
+        out_shape=jax.ShapeDtypeStruct((2, 1024, 512), F32),
+        in_specs=[in_hbm] * 3,
+        out_specs=in_hbm,
+        scratch_shapes=[
+            pltpu.VMEM((8, 2, 256, LANES), F32),
+            pltpu.VMEM((2, 2, 1024, LANES), F32),
+            pltpu.VMEM((2, 2, 1024, LANES), F32),
+            pltpu.VMEM((256, 768), BF16),
+            pltpu.SemaphoreType.DMA((8,)),
+            pltpu.SemaphoreType.DMA((6,)),
+        ],
+        compiler_params=pltpu.CompilerParams(vmem_limit_bytes=67043328),
+    )(late, ready, given[5])
 
 
 def solution(mesh):

time: 251 us -> 235 us (0.936)
  Pallas kernels: 246 us -> 235 us
  local copies, waits for them, and re-layouts: 4.64 us -> 0 us
    pallas_call x1 -> x2, Pallas kernels: 246 us -> 235 us  [the longest x1 229 us: local(): pl.pallas_call(kernel, out_shape=[jax.ShapeDtypeStruct((8, 2, 256, LANES)...]
    unnamed x1 -> x0, local copies, waits for them, and re-layouts: 4.64 us -> none
where the time goes in v2:
time: 235 us
  Pallas kernels  235 us (100%)
    pallas_call x1, Pallas kernels, local(): pl.pallas_call(kernel, out_shape=[jax.ShapeDtypeStruct((8, 2, 256, LANES)...  229 us
    pallas_call x1, Pallas kernels, local(): pl.pallas_call(last_kernel, out_shape=jax.ShapeDtypeStruct((2, 1024, 512)...  6 us

profile of v2, /device:TPU:1, one launch (start us, length us, event | category | flops | bytes accessed | tf_op | source)
XLA Modules:
  0.0 235.2 jit_solution(6917338061312351083)
XLA Ops:
  0.0 229.2 %shard_map.100 = (f32[8,2,256,128]{3,2,1,0:T(8,128)}, f32[2,2,1024,128]{3,2,1,0:T(8,128)}) custom-call(f32[2,32,16384]{2,1,0:T(8,128)} %voltage.1, f32[128,4096]{1,0:T(8,128)} %phase.1, f32[8,1024]{1,0:T(8,128)} %refs_0_.1, bf16[64,192]{1,0:T(8,128)(2,1)} %constant.14.clone.refs_1_, bf16[64,192]{1,0:T(8,128)(2,1)} %constant.15.clone.refs_2_, ...), custom_call_target="tpu_custom_call" | custom-call | tf_op jit(solution)/shard_map/pallas_call | solution.py:699
  229.2 6.0 %shard_map.101 = f32[2,1024,512]{2,1,0:T(8,128)} custom-call(f32[8,2,256,128]{3,2,1,0:T(8,128)} %get-tuple-element.7.late, f32[2,2,1024,128]{3,2,1,0:T(8,128)} %get-tuple-element.8.ready, bf16[256,768]{1,0:T(8,128)(2,1)} %constant.18.clone.refs_5_.lanes_out), custom_call_target="tpu_custom_call" | custom-call | tf_op jit(solution)/shard_map/pallas_call | solution.py:733

commit v3 on v2

--- a/solution.py
+++ b/solution.py
@@ -1,4 +1,5 @@
 import math
+import random
 
 import jax
 import jax.numpy as jnp
@@ -16,6 +17,12 @@
 LOG_TOTAL = 26
 GROUPS = DEVICES // 16
 CONSTANTS = 8
+FIRST_EDGE = 72
+FAR_FIRST = [
+    (n % 4, (n + n // 4) % 4, (n + n // 4 + n // 16) % 4, n // 64) for n in range(1, DEVICES)
+]
+random.Random(1).shuffle(FAR_FIRST)
+FAR_FIRST.sort(key=lambda offset: -sum(min(d, 4 - d) for d in offset[:3]))
 BY_MESH = pl.DeviceIdType.MESH
 F32 = jnp.float32
 BF16 = jnp.bfloat16
@@ -188,6 +195,8 @@
     wide,
     edge_send,
     edge_recv,
+    span_send,
+    span_recv,
     local_sem,
     sems1,
     sems2,
@@ -195,6 +204,7 @@
     sems4,
     phase_sem,
     edge_sem,
+    span_sem,
     send_sems,
     out_sem,
     given_sem,
@@ -489,128 +499,187 @@
     third_group(0, 15)
     lax.fori_loop(1, GROUPS, later_group, 0)
 
-    def fourth_part(turn, carry):
-        part = PARTS - 1 - turn
-        at = tile_rows(part)
+    def fourth_part(part):
+        at = slice(part * TILE, part * TILE + TILE)
 
         def load(n):
             return work[n, 0, at, :], work[n, 1, at, :]
 
         def finish(k, value):
-            send4[k, 0, at, :] = value[0]
-            send4[k, 1, at, :] = value[1]
+            for c in range(2):
+                send4[k, c, at, :] = value[c]
+                if part == 0:
+                    edge_send[k, c : c + 1, :] = value[c][TILE - 1 :]
 
         block_dft(load, tiles, finish, 1)
         recv4[me, :, at, :] = send4[me, :, at, :]
-        send_part(send4, recv4, part, send_sems.at[4], lambda step: sems4.at[part])
-        return carry
-
-    lax.fori_loop(0, PARTS, fourth_part, 0)
-
+
+    rows_of = [
+        [lax.rem(z + n, 4) * 8 for n in range(4)],
+        [lax.rem(y + n, 2) * 4 for n in range(4)],
+        [lax.rem(x + n, 4) for n in range(4)],
+    ]
+    cols_of = [
+        [lax.rem(y + n, 4) // 2 * 2 for n in range(4)],
+        [lax.rem(core + n, 2) for n in range(2)],
+    ]
+
+    def send4_part(part):
+        at = slice(part * TILE, part * TILE + TILE)
+        for dz, dy, dx, dc in FAR_FIRST:
+            to_row = rows_of[0][dz] + rows_of[1][dy] + rows_of[2][dx]
+            to_col = cols_of[0][dy] + cols_of[1][dc]
+            pltpu.make_async_remote_copy(
+                src_ref=send4.at[to_row * 4 + to_col, :, at, :],
+                dst_ref=recv4.at[me, :, at, :],
+                send_sem=send_sems.at[4],
+                recv_sem=sems4.at[part],
+                device_id=(to_row, to_col),
+                device_id_type=BY_MESH,
+            ).start()
+
+    def edge_pieces():
+        for dz, dy, dx, dc in FAR_FIRST:
+            to_row = rows_of[0][dz] + rows_of[1][dy] + rows_of[2][dx]
+            to_col = cols_of[0][dy] + cols_of[1][dc]
+            pltpu.make_async_remote_copy(
+                src_ref=edge_send.at[to_row * 4 + to_col],
+                dst_ref=edge_recv.at[me],
+                send_sem=send_sems.at[5],
+                recv_sem=edge_sem,
+                device_id=(to_row, to_col),
+                device_id_type=BY_MESH,
+            ).start()
+
+    with_edges = me >= FIRST_EDGE
+    fourth_part(3)
+    send4_part(3)
+    fourth_part(2)
+    send4_part(2)
+    fourth_part(1)
+    fourth_part(0)
+    pl.when(with_edges)(edge_pieces)
+    edge_recv[me] = edge_send[me]
+    send4_part(1)
     wait_part(recv4, sems4.at[3])
 
-    def edge_out(j, carry):
-        edge_send[j, 0:1, :] = recv4[72 + j, 0, ROWS - 1 : ROWS, :]
-        edge_send[j, 1:2, :] = recv4[72 + j, 1, ROWS - 1 : ROWS, :]
-        return carry
-
-    lax.fori_loop(0, 56, edge_out, 0)
+    def span_edge(j, carry):
+        span_send[j, 0:1, :] = recv4[FIRST_EDGE + j, 0, ROWS - 1 :, :]
+        span_send[j, 1:2, :] = recv4[FIRST_EDGE + j, 1, ROWS - 1 :, :]
+        return carry
+
+    lax.fori_loop(0, DEVICES - FIRST_EDGE, span_edge, 0)
     following = lax.rem(me + 1, DEVICES)
-    edge_copy = pltpu.make_async_remote_copy(
-        src_ref=edge_send,
-        dst_ref=edge_recv,
-        send_sem=send_sems.at[5],
-        recv_sem=edge_sem,
+    span_copy = pltpu.make_async_remote_copy(
+        src_ref=span_send,
+        dst_ref=span_recv,
+        send_sem=send_sems.at[6],
+        recv_sem=span_sem,
         device_id=(following // 4, lax.rem(following, 4)),
         device_id_type=BY_MESH,
     )
-    edge_copy.start()
+    span_copy.start()
+    send4_part(0)
+
     first_row = lax.broadcasted_iota(jnp.int32, (TILE, LANES), 0) == 0
     ahead = me > 0
-
-    def filter_half(half):
-        tile_list = (2 * half + 1, 2 * half)
-        tiles_out = all_tiles.at[half]
-
-        def one_position(high, part):
+    frames = table_a.reshape(PARTS, 8, 2, 128, LANES)
+    gathered = table_b.reshape(PARTS, 2, 1024, LANES)
+
+    def filter_part(part):
+        at = slice(part * TILE, part * TILE + TILE)
+
+        def edge_row(high, m, c):
+            if part == 0:
+                edge = span_recv[8 * m + high - FIRST_EDGE, c : c + 1, :]
+                return jnp.where(ahead, edge, 0.0)
+            if part == 1:
+                return edge_recv[8 * m + high, c : c + 1, :]
+            return recv4[8 * m + high, c, part * TILE - 1 : part * TILE, :]
+
+        def one_position(high, carry):
             weights = [
                 taps[t : t + 1, pl.ds(pl.multiple_of(high * LANES, LANES), LANES)]
                 for t in range(8)
             ]
-            at = slice(part * TILE, part * TILE + TILE)
             for c in range(2):
                 now = [recv4[8 * m + high, c, at, :] for m in range(16)]
                 old = [None] * 16
                 for m in range(9, 16):
-                    shifted = pltpu.roll(now[m], 1, 0)
-                    if part == 0:
-                        edge = edge_recv[8 * (m - 9) + high, c : c + 1, :]
-                        edge = jnp.where(ahead, edge, 0.0)
-                    else:
-                        edge = recv4[8 * m + high, c, part * TILE - 1 : part * TILE, :]
-                    old[m] = jnp.where(first_row, edge, shifted)
+                    old[m] = jnp.where(first_row, edge_row(high, m, c), pltpu.roll(now[m], 1, 0))
                 for m in range(16):
                     total = weights[0] * now[m]
                     for t in range(1, 8):
                         total = total + weights[t] * (now[m - t] if m >= t else old[m - t + 16])
                     work[16 * high + m, c, at, :] = total
-
-        for part in tile_list:
-            if part == 0:
-                edge_copy.wait_recv()
-
-            def position_of(high, carry, part=part):
-                one_position(high, part)
-                return carry
-
-            lax.fori_loop(0, 8, position_of, 0)
+            return carry
+
+        lax.fori_loop(0, 8, one_position, 0)
 
         def one_frame(m, carry):
-            for part in tile_list:
-                at_tile = part % 2
-                at = slice(part * TILE, part * TILE + TILE)
-                values = small_dft(
-                    [(work[16 * high + m, 0, at, :], work[16 * high + m, 1, at, :]) for high in range(8)],
-                    -1,
-                )
-                for a, value in enumerate(values):
-                    value = times(value, (out_turn[0, a : a + 1, :], out_turn[1, a : a + 1, :]))
-                    for c in range(2):
-                        tiles_out[a, c, pl.ds(128 * at_tile + m, TILE, stride=16), :] = value[c]
+            values = small_dft(
+                [(work[16 * high + m, 0, at, :], work[16 * high + m, 1, at, :]) for high in range(8)],
+                -1,
+            )
+            for a, value in enumerate(values):
+                value = times(value, (out_turn[0, a : a + 1, :], out_turn[1, a : a + 1, :]))
+                for c in range(2):
+                    frames[part, a, c, pl.ds(m, TILE, stride=16), :] = value[c]
             return carry
 
         lax.fori_loop(0, 16, one_frame, 0)
 
-        if half == 0:
-            return
-
-        def one_class(a, carry):
-            both = frames_dft(lanes_out, tiles_out[a, 0], tiles_out[a, 1])
+    def ready_copy(part):
+        return pltpu.make_async_copy(gathered.at[part], ready.at[part - 1], out_sem.at[part])
+
+    def finish_parts(parts):
+        classes = 2 // len(parts)
+
+        def some_classes(step, carry):
+            each = [(p, classes * step + n) for n in range(classes) for p in parts]
+            both = frames_dft(
+                lanes_out, *[jnp.concatenate([frames[p, a, c] for p, a in each]) for c in range(2)]
+            )
             for c in range(2):
-                for side in range(2):
-                    gathered[side, c, pl.ds(a, 128, stride=8), :] = both[
-                        c * 128 : c * 128 + 128, side * LANES : side * LANES + LANES
+                for n, (p, a) in enumerate(each):
+                    gathered[p, c, pl.ds(a, 128, stride=8), :] = both[
+                        c * 128 : c * 128 + 128, n * LANES : n * LANES + LANES
                     ]
             return carry
 
-        lax.fori_loop(0, 8, one_class, 0)
-        ready_copy.start()
-
-    all_tiles = table_a.reshape(2, 8, 2, 256, LANES)
-    gathered = table_b.reshape(4, 2, 1024, LANES).at[pl.ds(0, 2)]
-    ready_copy = pltpu.make_async_copy(gathered, ready, out_sem.at[0])
-    late_copy = pltpu.make_async_copy(all_tiles.at[0], late, out_sem.at[1])
+        lax.fori_loop(0, 8 // classes, some_classes, 0)
+        for p in parts:
+            ready_copy(p).start()
 
     wait_part(recv4, sems4.at[2])
+    filter_part(3)
     wait_part(recv4, sems4.at[1])
-    filter_half(1)
+    filter_part(2)
+    finish_parts((2, 3))
+
+    def wait_edges(count):
+        ref = edge_recv.at[pl.ds(0, count)]
+        pltpu.make_async_copy(ref, ref, edge_sem).wait()
+
+    pl.when(with_edges)(lambda: wait_edges(DEVICES - FIRST_EDGE - 1))
+    pl.when(jnp.logical_not(with_edges))(lambda: wait_edges(DEVICES - FIRST_EDGE))
+    filter_part(1)
+    finish_parts((1,))
     wait_part(recv4, sems4.at[0])
-    filter_half(0)
-
+    span_copy.wait_recv()
+    filter_part(0)
+    late_copy = pltpu.make_async_copy(frames.at[0], late, out_sem.at[0])
     late_copy.start()
-    ready_copy.wait()
+    for part in range(1, PARTS):
+        ready_copy(part).wait()
     late_copy.wait()
-    edge_copy.wait_send()
+    span_copy.wait_send()
+
+    def wait_edges_sent():
+        ref = edge_recv.at[pl.ds(0, DEVICES - 1)]
+        pltpu.make_async_copy(ref, ref, send_sems.at[5]).wait()
+
+    pl.when(with_edges)(wait_edges_sent)
     pieces = recv1.at[pl.ds(0, DEVICES - 1)]
     for at in (0, 2, 3, 4):
         pltpu.make_async_copy(pieces, pieces, send_sems.at[at]).wait()
@@ -620,35 +689,35 @@
 def last_kernel(late, ready, lanes_out, result, frames, passing, gathered, matrix, sems, more):
     frame_copies = [pltpu.make_async_copy(late.at[a], frames.at[a], sems.at[a]) for a in range(8)]
     matrix_copy = pltpu.make_async_copy(lanes_out, matrix, more.at[0])
-    pass_in = pltpu.make_async_copy(ready, passing, more.at[1])
-
-    def to_result(source, side, column, sem):
-        return pltpu.make_async_copy(
-            source.at[side], result.at[:, :, pl.ds(column * LANES, LANES)], sem
+    pass_in = [
+        pltpu.make_async_copy(ready.at[n], passing.at[n], more.at[1 + n]) for n in range(3)
+    ]
+
+    def to_result(source, column, sem):
+        return pltpu.make_async_copy(source, result.at[:, :, pl.ds(column * LANES, LANES)], sem)
+
+    passed = [to_result(passing.at[n], 1 + n, more.at[4 + n]) for n in range(3)]
+    computed = to_result(gathered, 0, more.at[7])
+    matrix_copy.start()
+    for copy in frame_copies + pass_in:
+        copy.start()
+    matrix_copy.wait()
+    for a in range(0, 8, 2):
+        frame_copies[a].wait()
+        frame_copies[a + 1].wait()
+        both = frames_dft(
+            matrix, *[jnp.concatenate([frames[a, c], frames[a + 1, c]]) for c in range(2)]
         )
-
-    passed = [to_result(passing, side, 2 + side, more.at[2 + side]) for side in range(2)]
-    computed = [to_result(gathered, side, side, more.at[4 + side]) for side in range(2)]
-    matrix_copy.start()
-    for copy in frame_copies:
-        copy.start()
-    pass_in.start()
-    matrix_copy.wait()
-    for a in range(8):
-        frame_copies[a].wait()
-        both = frames_dft(matrix, frames[a, 0], frames[a, 1])
         for c in range(2):
-            for side in range(2):
-                gathered[side, c, pl.ds(a, 128, stride=8), :] = both[
-                    c * 128 : c * 128 + 128, side * LANES : side * LANES + LANES
+            for n in range(2):
+                gathered[c, pl.ds(a + n, 128, stride=8), :] = both[
+                    c * 128 : c * 128 + 128, n * LANES : n * LANES + LANES
                 ]
-        if a == 3:
-            pass_in.wait()
-            for copy in passed:
-                copy.start()
-    for copy in computed:
-        copy.start()
-    for copy in passed + computed:
+        if a < 6:
+            pass_in[a // 2].wait()
+            passed[a // 2].start()
+    computed.start()
+    for copy in passed + [computed]:
         copy.wait()
 
 
@@ -699,8 +768,8 @@
     late, ready = pl.pallas_call(
         kernel,
         out_shape=[
-            jax.ShapeDtypeStruct((8, 2, 256, LANES), F32),
-            jax.ShapeDtypeStruct((2, 2, 1024, LANES), F32),
+            jax.ShapeDtypeStruct((8, 2, 128, LANES), F32),
+            jax.ShapeDtypeStruct((3, 2, 1024, LANES), F32),
         ],
         in_specs=[in_hbm] * (2 + len(given)),
         out_specs=[in_hbm] * 2,
@@ -712,8 +781,10 @@
         + [
             pltpu.VMEM((DEVICES, 2, TILE, LANES), F32),
             pltpu.VMEM((DEVICES, TILE, 2 * LANES), F32),
-            pltpu.VMEM((56, 2, LANES), F32),
-            pltpu.VMEM((56, 2, LANES), F32),
+            pltpu.VMEM((DEVICES, 2, LANES), F32),
+            pltpu.VMEM((DEVICES, 2, LANES), F32),
+            pltpu.VMEM((DEVICES - FIRST_EDGE, 2, LANES), F32),
+            pltpu.VMEM((DEVICES - FIRST_EDGE, 2, LANES), F32),
             pltpu.SemaphoreType.DMA((2,)),
             pltpu.SemaphoreType.DMA((PARTS,)),
             pltpu.SemaphoreType.DMA((PARTS,)),
@@ -721,8 +792,9 @@
             pltpu.SemaphoreType.DMA((PARTS,)),
             pltpu.SemaphoreType.DMA,
             pltpu.SemaphoreType.DMA,
-            pltpu.SemaphoreType.DMA((6,)),
-            pltpu.SemaphoreType.DMA((2,)),
+            pltpu.SemaphoreType.DMA,
+            pltpu.SemaphoreType.DMA((7,)),
+            pltpu.SemaphoreType.DMA((PARTS,)),
             pltpu.SemaphoreType.DMA((CONSTANTS,)),
             pltpu.SemaphoreType.REGULAR,
         ],
@@ -736,12 +808,12 @@
         in_specs=[in_hbm] * 3,
         out_specs=in_hbm,
         scratch_shapes=[
-            pltpu.VMEM((8, 2, 256, LANES), F32),
-            pltpu.VMEM((2, 2, 1024, LANES), F32),
-            pltpu.VMEM((2, 2, 1024, LANES), F32),
+            pltpu.VMEM((8, 2, 128, LANES), F32),
+            pltpu.VMEM((3, 2, 1024, LANES), F32),
+            pltpu.VMEM((2, 1024, LANES), F32),
             pltpu.VMEM((256, 768), BF16),
             pltpu.SemaphoreType.DMA((8,)),
-            pltpu.SemaphoreType.DMA((6,)),
+            pltpu.SemaphoreType.DMA((8,)),
         ],
         compiler_params=pltpu.CompilerParams(vmem_limit_bytes=67043328),
     )(late, ready, given[5])

time: 235 us -> 232 us (0.987)
  Pallas kernels: 235 us -> 232 us
where the time goes in v3:
time: 232 us
  Pallas kernels  232 us (100%)
    pallas_call x1, Pallas kernels, local(): pl.pallas_call(kernel, out_shape=[jax.ShapeDtypeStruct((8, 2, 128, LANES)...  228 us

profile of v3, /device:TPU:1, one launch (start us, length us, event | category | flops | bytes accessed | tf_op | source)
XLA Modules:
  0.0 231.9 jit_solution(627350640657423533)
XLA Ops:
  0.0 227.9 %shard_map.100 = (f32[8,2,128,128]{3,2,1,0:T(8,128)}, f32[3,2,1024,128]{3,2,1,0:T(8,128)}) custom-call(f32[2,32,16384]{2,1,0:T(8,128)} %voltage.1, f32[128,4096]{1,0:T(8,128)} %phase.1, f32[8,1024]{1,0:T(8,128)} %refs_0_.1, bf16[64,192]{1,0:T(8,128)(2,1)} %constant.14.clone.refs_1_, bf16[64,192]{1,0:T(8,128)(2,1)} %constant.15.clone.refs_2_, ...), custom_call_target="tpu_custom_call" | custom-call | tf_op jit(solution)/shard_map/pallas_call | solution.py:768
  227.9 4.0 %shard_map.101 = f32[2,1024,512]{2,1,0:T(8,128)} custom-call(f32[8,2,128,128]{3,2,1,0:T(8,128)} %get-tuple-element.7.late, f32[3,2,1024,128]{3,2,1,0:T(8,128)} %get-tuple-element.8.ready, bf16[256,768]{1,0:T(8,128)(2,1)} %constant.18.clone.refs_5_.lanes_out), custom_call_target="tpu_custom_call" | custom-call | tf_op jit(solution)/shard_map/pallas_call | solution.py:805

commit v4 on v3

--- a/solution.py
+++ b/solution.py
@@ -14,13 +14,16 @@
 TILE = 8
 PARTS = ROWS // TILE
 LANES = 128
+HALF = LANES // 2
 LOG_TOTAL = 26
 GROUPS = DEVICES // 16
-CONSTANTS = 8
+CONSTANTS = 9
 FIRST_EDGE = 72
-FAR_FIRST = [
-    (n % 4, (n + n // 4) % 4, (n + n // 4 + n // 16) % 4, n // 64) for n in range(1, DEVICES)
+IN_STEPS = [
+    (n % 4, (n % 4 + n // 4) % 4, (n % 4 + n // 4 + n // 16) % 4, n // 64)
+    for n in range(1, DEVICES)
 ]
+FAR_FIRST = list(IN_STEPS)
 random.Random(1).shuffle(FAR_FIRST)
 FAR_FIRST.sort(key=lambda offset: -sum(min(d, 4 - d) for d in offset[:3]))
 BY_MESH = pl.DeviceIdType.MESH
@@ -49,16 +52,12 @@
     return a[0] * b[0] - a[1] * b[1], a[0] * b[1] + a[1] * b[0]
 
 
-def times_conj(a, b):
-    return a[0] * b[0] + a[1] * b[1], a[1] * b[0] - a[0] * b[1]
-
-
 def plus(a, b):
-    return a[0] + b[0], a[1] + b[1]
+    return tuple(x + y for x, y in zip(a, b))
 
 
 def minus(a, b):
-    return a[0] - b[0], a[1] - b[1]
+    return tuple(x - y for x, y in zip(a, b))
 
 
 def turned(a, part, whole, sign):
@@ -84,8 +83,35 @@
     return a[0] * cos_part - a[1] * sin_part, a[0] * sin_part + a[1] * cos_part
 
 
+def lane_sign(shape):
+    return jnp.where(lax.broadcasted_iota(jnp.int32, shape, len(shape) - 1) < HALF, -1.0, 1.0)
+
+
+def swapped(x):
+    return pltpu.roll(x, HALF, x.ndim - 1)
+
+
+def packed_times(x, turn):
+    return x * turn[0] + swapped(x) * turn[1]
+
+
+def packed_turned(a, part, whole, sign):
+    part = part % whole
+    angle = sign * 2.0 * math.pi * part / whole
+    (x,) = a
+    if part == 0:
+        return a
+    if 2 * part == whole:
+        return (-x,)
+    if 4 * part in (whole, 3 * whole):
+        up = (4 * part == whole) == (sign > 0)
+        return (swapped(x) * (lane_sign(x.shape) if up else -lane_sign(x.shape)),)
+    return (math.cos(angle) * x + swapped(x) * (math.sin(angle) * lane_sign(x.shape)),)
+
+
 def small_dft(xs, sign):
     n = len(xs)
+    turn = turned if len(xs[0]) == 2 else packed_turned
     if n == 1:
         return xs
     if n == 2:
@@ -93,9 +119,9 @@
     parts = [small_dft(xs[r::4], sign) for r in range(4)]
     out = [None] * n
     for k in range(n // 4):
-        a, b, c, d = (turned(parts[r][k], r * k, n, sign) for r in range(4))
+        a, b, c, d = (turn(parts[r][k], r * k, n, sign) for r in range(4))
         ac, bd = plus(a, c), plus(b, d)
-        ac_, bd_ = minus(a, c), turned(minus(b, d), 1, 4, sign)
+        ac_, bd_ = minus(a, c), turn(minus(b, d), 1, 4, sign)
         out[k] = plus(ac, bd)
         out[k + n // 4] = plus(ac_, bd_)
         out[k + n // 2] = minus(ac, bd)
@@ -107,19 +133,25 @@
     for low in range(8):
         values = small_dft([load(8 * high + low) for high in range(16)], sign)
         for k, value in enumerate(values):
-            value = turned(value, low * k, 128, sign)
-            scratch[8 * k + low, 0] = value[0]
-            scratch[8 * k + low, 1] = value[1]
-
-    def second(k, carry):
-        values = small_dft(
-            [(scratch[8 * k + low, 0], scratch[8 * k + low, 1]) for low in range(8)], sign
-        )
-        for high, value in enumerate(values):
-            finish(k + 16 * high, value)
-        return carry
-
-    lax.fori_loop(0, 16, second, 0)
+            turn = turned if len(value) == 2 else packed_turned
+            value = turn(value, low * k, 128, sign)
+            for c, x in enumerate(value):
+                scratch[8 * k + low, c] = x
+    parts = range(len(value))
+    together = 1 if len(value) == 2 else 4
+
+    def second(step, carry):
+        ks = [together * step + n for n in range(together)]
+        given = [
+            [tuple(scratch[8 * k + low, c] for c in parts) for low in range(8)] for k in ks
+        ]
+        done = [small_dft(values, sign) for values in given]
+        for k, values in zip(ks, done):
+            for high, value in enumerate(values):
+                finish(k + 16 * high, value)
+        return carry
+
+    lax.fori_loop(0, 16 // together, second, 0)
 
 
 def quarter_sincos(angle, quarter):
@@ -175,7 +207,7 @@
     given, refs = refs[:CONSTANTS], refs[CONSTANTS:]
     late, ready, refs = refs[0], refs[1], refs[2:]
     held, refs = refs[:CONSTANTS], refs[CONSTANTS:]
-    taps, rows_fwd, rows_inv, lanes_fwd, lanes_inv, lanes_out, mid_turn, out_turn = held
+    taps, rows_fwd, rows_inv, lanes_fwd, lanes_inv, lanes_out, mid_turn, mid_back, out_turn = held
     (
     recv1,
     work,
@@ -197,6 +229,7 @@
     edge_recv,
     span_send,
     span_recv,
+    half_taps,
     local_sem,
     sems1,
     sems2,
@@ -204,7 +237,7 @@
     sems4,
     phase_sem,
     edge_sem,
-    span_sem,
+    span_sems,
     send_sems,
     out_sem,
     given_sem,
@@ -256,16 +289,43 @@
         pl.semaphore_signal(plane_sem, **greet_along(other))
     pl.semaphore_wait(plane_sem, 3)
 
-    def send_piece(step, source_of, target, send_sem, recv_sem):
-        to_row, to_col = partner(place, step)
-        pltpu.make_async_remote_copy(
-            src_ref=source_of(to_row * 4 + to_col),
-            dst_ref=target,
-            send_sem=send_sem,
-            recv_sem=recv_sem,
-            device_id=(to_row, to_col),
-            device_id_type=BY_MESH,
-        ).start()
+    rows_of = [
+        [lax.rem(z + n, 4) * 8 for n in range(4)],
+        [lax.rem(y + n, 2) * 4 for n in range(4)],
+        [lax.rem(x + n, 4) for n in range(4)],
+    ]
+    cols_of = [
+        [lax.rem(y + n, 4) // 2 * 2 for n in range(4)],
+        [lax.rem(core + n, 2) for n in range(2)],
+    ]
+
+    def send_loop(source_of, target, send_sem, recv_sem):
+        def one(step, carry):
+            to_row, to_col = partner(place, step)
+            pltpu.make_async_remote_copy(
+                src_ref=source_of(to_row * 4 + to_col),
+                dst_ref=target,
+                send_sem=send_sem,
+                recv_sem=recv_sem,
+                device_id=(to_row, to_col),
+                device_id_type=BY_MESH,
+            ).start()
+            return carry
+
+        lax.fori_loop(1, DEVICES, one, 0)
+
+    def send_all(order, source_of, target, send_sem, recv_sem_of):
+        for n, (dz, dy, dx, dc) in enumerate(order):
+            to_row = rows_of[0][dz] + rows_of[1][dy] + rows_of[2][dx]
+            to_col = cols_of[0][dy] + cols_of[1][dc]
+            pltpu.make_async_remote_copy(
+                src_ref=source_of(to_row * 4 + to_col),
+                dst_ref=target,
+                send_sem=send_sem,
+                recv_sem=recv_sem_of(n + 1),
+                device_id=(to_row, to_col),
+                device_id_type=BY_MESH,
+            ).start()
 
     def tile_rows(part):
         return pl.ds(pl.multiple_of(part * TILE, TILE), TILE)
@@ -275,19 +335,14 @@
         pltpu.make_async_copy(ref, ref, sem).wait()
 
     def voltage_part(part, carry):
-        def one(step, inner):
-            send_piece(
-                step,
-                lambda to: voltage.at[
-                    :, tile_rows(part), pl.ds(pl.multiple_of(to * LANES, LANES), LANES)
-                ],
-                recv1.at[me, :, tile_rows(part), :],
-                send_sems.at[0],
-                sems1.at[part],
-            )
-            return inner
-
-        lax.fori_loop(1, DEVICES, one, 0)
+        send_loop(
+            lambda to: voltage.at[
+                :, tile_rows(part), pl.ds(pl.multiple_of(to * LANES, LANES), LANES)
+            ],
+            recv1.at[me, :, tile_rows(part), :],
+            send_sems.at[0],
+            sems1.at[part],
+        )
         return carry
 
     lax.fori_loop(0, PARTS, voltage_part, 0)
@@ -301,13 +356,12 @@
 
     lax.fori_loop(0, ROWS, phase_out, 0)
 
-    def phase_piece(step, carry):
-        send_piece(
-            step, lambda to: phase_send.at[to], phase_recv.at[me], send_sems.at[1], phase_sem
-        )
-        return carry
-
-    lax.fori_loop(1, DEVICES, phase_piece, 0)
+    send_loop(
+        lambda to: phase_send.at[to],
+        phase_recv.at[me],
+        send_sems.at[1],
+        phase_sem,
+    )
     phase_recv[me] = phase_send[me]
 
     def fill(a, carry):
@@ -344,49 +398,49 @@
     for copy in given_copies:
         copy.wait()
 
-    def row_dft(matrix, first, second):
-        high, low = halves(
-            jnp.concatenate([first.reshape(64, LANES), second.reshape(64, LANES)], axis=1)
-        )
+    first_lanes = lax.broadcasted_iota(jnp.int32, (8, LANES), 1) < HALF
+    for high in range(8):
+        columns = slice(high * LANES, high * LANES + LANES)
+        straight = taps[:, columns]
+        half_taps[0, :, columns] = jnp.where(first_lanes, straight, swapped(straight))
+        half_taps[1, :, columns] = jnp.where(first_lanes, swapped(straight), straight)
+
+    def split_dot(matrix, columns):
+        high, low = halves(columns)
         return jnp.dot(
             matrix[...],
             jnp.concatenate([high, low, high], axis=0),
             preferred_element_type=F32,
         )
 
-    def row_dfts(matrix, source, places):
+    def in_pairs(places):
+        return zip(places[::2], places[1::2])
+
+    def second_step(group, carry):
         done = []
-        for first, second in zip(places[::2], places[1::2]):
-            both = row_dft(matrix, source[first], source[second])
-            done.append((first, (both[:ROWS, :LANES], both[ROWS:, :LANES])))
-            done.append((second, (both[:ROWS, LANES:], both[ROWS:, LANES:])))
-        return done
-
-    def second_step(group, carry):
-        for at, value in row_dfts(rows_fwd, work, [8 * group + n for n in range(8)]):
-            value = times(value, (table_b[at, 0], table_b[at, 1]))
-            send2[at, 0] = value[0]
-            send2[at, 1] = value[1]
-        return carry
-
-    def send_part(buffer, target, part, send_sem, recv_sem_of):
-        def one(step, inner):
-            send_piece(
-                step,
-                lambda to: buffer.at[to, :, tile_rows(part), :],
-                target.at[me, :, tile_rows(part), :],
-                send_sem,
-                recv_sem_of(step),
+        for pair in in_pairs([8 * group + n for n in range(8)]):
+            both = split_dot(
+                rows_fwd, jnp.concatenate([work[a].reshape(64, LANES) for a in pair], axis=1)
             )
-            return inner
-
-        lax.fori_loop(1, DEVICES, one, 0)
+            for n, a in enumerate(pair):
+                columns = slice(n * LANES, n * LANES + LANES)
+                done.append((a, (both[:ROWS, columns], both[ROWS:, columns])))
+        for a, value in done:
+            value = times(value, (table_b[a, 0], table_b[a, 1]))
+            send2[a, 0] = value[0]
+            send2[a, 1] = value[1]
+        return carry
 
     lax.fori_loop(0, DEVICES // 8, second_step, 0)
     recv2[me] = send2[me]
 
     def send2_part(part, carry):
-        send_part(send2, recv2, part, send_sems.at[2], lambda step: sems2.at[part])
+        send_loop(
+            lambda to: send2.at[to, :, tile_rows(part), :],
+            recv2.at[me, :, tile_rows(part), :],
+            send_sems.at[2],
+            sems2.at[part],
+        )
         return carry
 
     lax.fori_loop(0, PARTS, send2_part, 0)
@@ -403,10 +457,15 @@
 
     lax.fori_loop(0, ROWS, phase_back, 0)
 
+    back_tables = table_b, work
+    sign = lane_sign((ROWS, LANES))
+
     def refill(h, carry):
-        cos_part, sin_part = unit((me + 128 * sublane) * (128 * h + lane), LOG_TOTAL)
-        table_b[h, 0] = cos_part
-        table_b[h, 1] = sin_part
+        for half in range(2):
+            at = 128 * h + HALF * half + (lane & (HALF - 1))
+            cos_part, sin_part = unit((me + 128 * sublane) * at, LOG_TOTAL)
+            back_tables[half][h, 0] = cos_part
+            back_tables[half][h, 1] = sin_part * sign
         return carry
 
     lax.fori_loop(0, DEVICES, refill, 0)
@@ -450,184 +509,208 @@
 
         lax.fori_loop(0, 4, lanes_step, 0)
 
-        def load_back(n):
-            turn = mid_turn[0, pl.ds(n, 1), :], mid_turn[1, pl.ds(n, 1), :]
-            return times_conj((wide[n, :, :LANES], wide[n, :, LANES:]), turn)
-
-        def finish_back(k, value):
-            value = times(value, (table_b[k, 0, at, :], table_b[k, 1, at, :]))
-            send3[k, 0, at, :] = value[0]
-            send3[k, 1, at, :] = value[1]
-
-        block_dft(load_back, tiles, finish_back, 1)
-        recv3[me, :, at, :] = send3[me, :, at, :]
-        send_part(
-            send3, recv3, part, send_sems.at[3], lambda step: sems3.at[GROUPS * part + step // 16]
+        for half in range(2):
+            columns = slice(half * LANES, half * LANES + LANES)
+
+            def load_back(n, half=half, columns=columns):
+                turn = mid_back[2 * half, pl.ds(n, 1), :], mid_back[2 * half + 1, pl.ds(n, 1), :]
+                return (packed_times(wide[n, :, columns], turn),)
+
+            def finish_back(k, value, half=half):
+                table = back_tables[half]
+                send3[k, half, at, :] = packed_times(
+                    value[0], (table[k, 0, at, :], table[k, 1, at, :])
+                )
+
+            block_dft(load_back, tiles, finish_back, 1)
+            recv3[me, half, at, :] = send3[me, half, at, :]
+        send3_part(0, part)
+        return carry
+
+    def send3_part(half, part):
+        send_all(
+            IN_STEPS,
+            lambda to: send3.at[to, half, tile_rows(part), :],
+            recv3.at[me, half, tile_rows(part), :],
+            send_sems.at[3],
+            lambda n: sems3.at[(half * PARTS + part) * GROUPS + n // 16],
         )
+
+    def send3_later(part, carry):
+        send3_part(1, part)
         return carry
 
     lax.fori_loop(0, PARTS, middle_part, 0)
-
-    def third_step(group, half):
+    lax.fori_loop(0, PARTS, send3_later, 0)
+
+    def third_step(half, group, eighth):
         places = []
         for n in range(8):
-            from_row, from_col = partner(place, 16 * group + 8 * half + n, 3)
+            from_row, from_col = partner(place, 16 * group + 8 * eighth + n, 3)
             places.append(from_row * 4 + from_col)
-        for at, value in row_dfts(rows_inv, recv3, places):
-            value = times_conj(value, (table_a[at, 0], table_a[at, 1]))
-            work[at, 0] = value[0]
-            work[at, 1] = value[1]
-
-    def third_group(group, count):
+        done = []
+        for pair in in_pairs(places):
+            straight = [recv3[a, half] for a in pair]
+            turned_up = [swapped(value) * sign for value in straight]
+            both = split_dot(
+                rows_inv,
+                jnp.concatenate(
+                    [jnp.concatenate(straight, axis=1), jnp.concatenate(turned_up, axis=1)], axis=0
+                ),
+            )
+            for n, a in enumerate(pair):
+                done.append((a, both[:, n * LANES : n * LANES + LANES]))
+        for a, value in done:
+            work[a, half] = packed_times(value, (table_a[a, 0], -sign * table_a[a, 1]))
+
+    def third_group(half, group, count):
         def wait_one(part, inner):
-            ref = recv3.at[pl.ds(0, count), :, pl.ds(0, TILE), :]
-            pltpu.make_async_copy(ref, ref, sems3.at[GROUPS * part + group]).wait()
+            ref = recv3.at[pl.ds(0, count), half, pl.ds(0, TILE), :]
+            pltpu.make_async_copy(
+                ref, ref, sems3.at[(half * PARTS + part) * GROUPS + group]
+            ).wait()
             return inner
 
         lax.fori_loop(0, PARTS, wait_one, 0)
 
-        def one(half, inner):
-            third_step(group, half)
+        def one(eighth, inner):
+            third_step(half, group, eighth)
             return inner
 
         lax.fori_loop(0, 2, one, 0)
 
-    def later_group(group, carry):
-        third_group(group, 16)
-        return carry
-
-    third_group(0, 15)
-    lax.fori_loop(1, GROUPS, later_group, 0)
-
-    def fourth_part(part):
+    def third_half(half):
+        def later_group(group, carry):
+            third_group(half, group, 16)
+            return carry
+
+        third_group(half, 0, 15)
+        lax.fori_loop(1, GROUPS, later_group, 0)
+
+    def fourth_part(half, part):
         at = slice(part * TILE, part * TILE + TILE)
 
         def load(n):
-            return work[n, 0, at, :], work[n, 1, at, :]
+            return (work[n, half, at, :],)
 
         def finish(k, value):
-            for c in range(2):
-                send4[k, c, at, :] = value[c]
-                if part == 0:
-                    edge_send[k, c : c + 1, :] = value[c][TILE - 1 :]
+            send4[k, half, at, :] = value[0]
+            if (half, part) in ((1, 0), (1, 1)):
+                edge_send[k, part : part + 1, :] = value[0][TILE - 1 :]
 
         block_dft(load, tiles, finish, 1)
-        recv4[me, :, at, :] = send4[me, :, at, :]
-
-    rows_of = [
-        [lax.rem(z + n, 4) * 8 for n in range(4)],
-        [lax.rem(y + n, 2) * 4 for n in range(4)],
-        [lax.rem(x + n, 4) for n in range(4)],
+        recv4[me, half, at, :] = send4[me, half, at, :]
+
+    def send4_part(half, part):
+        at = slice(part * TILE, part * TILE + TILE)
+        send_all(
+            FAR_FIRST,
+            lambda to: send4.at[to, half, at, :],
+            recv4.at[me, half, at, :],
+            send_sems.at[4],
+            lambda n: sems4.at[half * PARTS + part],
+        )
+
+    def edge_pieces():
+        send_all(
+            FAR_FIRST,
+            lambda to: edge_send.at[to],
+            edge_recv.at[me],
+            send_sems.at[5],
+            lambda n: edge_sem,
+        )
+
+    def wait4(half, part):
+        ref = recv4.at[pl.ds(0, DEVICES - 1), half, pl.ds(0, TILE), :]
+        pltpu.make_async_copy(ref, ref, sems4.at[half * PARTS + part]).wait()
+
+    following = lax.rem(me + 1, DEVICES)
+    span_copies = [
+        pltpu.make_async_remote_copy(
+            src_ref=span_send.at[half],
+            dst_ref=span_recv.at[half],
+            send_sem=send_sems.at[6 + half],
+            recv_sem=span_sems.at[half],
+            device_id=(following // 4, lax.rem(following, 4)),
+            device_id_type=BY_MESH,
+        )
+        for half in range(2)
     ]
-    cols_of = [
-        [lax.rem(y + n, 4) // 2 * 2 for n in range(4)],
-        [lax.rem(core + n, 2) for n in range(2)],
-    ]
-
-    def send4_part(part):
-        at = slice(part * TILE, part * TILE + TILE)
-        for dz, dy, dx, dc in FAR_FIRST:
-            to_row = rows_of[0][dz] + rows_of[1][dy] + rows_of[2][dx]
-            to_col = cols_of[0][dy] + cols_of[1][dc]
-            pltpu.make_async_remote_copy(
-                src_ref=send4.at[to_row * 4 + to_col, :, at, :],
-                dst_ref=recv4.at[me, :, at, :],
-                send_sem=send_sems.at[4],
-                recv_sem=sems4.at[part],
-                device_id=(to_row, to_col),
-                device_id_type=BY_MESH,
-            ).start()
-
-    def edge_pieces():
-        for dz, dy, dx, dc in FAR_FIRST:
-            to_row = rows_of[0][dz] + rows_of[1][dy] + rows_of[2][dx]
-            to_col = cols_of[0][dy] + cols_of[1][dc]
-            pltpu.make_async_remote_copy(
-                src_ref=edge_send.at[to_row * 4 + to_col],
-                dst_ref=edge_recv.at[me],
-                send_sem=send_sems.at[5],
-                recv_sem=edge_sem,
-                device_id=(to_row, to_col),
-                device_id_type=BY_MESH,
-            ).start()
+
+    def send_span(half):
+        def span_row(j, carry):
+            span_send[half, pl.ds(j, 1), :] = recv4[FIRST_EDGE + j, half, ROWS - 1 :, :]
+            return carry
+
+        wait4(half, 3)
+        lax.fori_loop(0, DEVICES - FIRST_EDGE, span_row, 0)
+        span_copies[half].start()
 
     with_edges = me >= FIRST_EDGE
-    fourth_part(3)
-    send4_part(3)
-    fourth_part(2)
-    send4_part(2)
-    fourth_part(1)
-    fourth_part(0)
+    third_half(0)
+    for part in (3, 2, 1, 0):
+        fourth_part(0, part)
+        send4_part(0, part)
+    third_half(1)
+    for part in (3, 2, 1, 0):
+        fourth_part(1, part)
+    edge_recv[me] = edge_send[me]
+    send_span(0)
+    send4_part(1, 3)
     pl.when(with_edges)(edge_pieces)
-    edge_recv[me] = edge_send[me]
-    send4_part(1)
-    wait_part(recv4, sems4.at[3])
-
-    def span_edge(j, carry):
-        span_send[j, 0:1, :] = recv4[FIRST_EDGE + j, 0, ROWS - 1 :, :]
-        span_send[j, 1:2, :] = recv4[FIRST_EDGE + j, 1, ROWS - 1 :, :]
-        return carry
-
-    lax.fori_loop(0, DEVICES - FIRST_EDGE, span_edge, 0)
-    following = lax.rem(me + 1, DEVICES)
-    span_copy = pltpu.make_async_remote_copy(
-        src_ref=span_send,
-        dst_ref=span_recv,
-        send_sem=send_sems.at[6],
-        recv_sem=span_sem,
-        device_id=(following // 4, lax.rem(following, 4)),
-        device_id_type=BY_MESH,
-    )
-    span_copy.start()
-    send4_part(0)
+    send4_part(1, 2)
+    send4_part(1, 1)
 
     first_row = lax.broadcasted_iota(jnp.int32, (TILE, LANES), 0) == 0
     ahead = me > 0
     frames = table_a.reshape(PARTS, 8, 2, 128, LANES)
     gathered = table_b.reshape(PARTS, 2, 1024, LANES)
 
-    def filter_part(part):
+    def filter_part(half, part):
         at = slice(part * TILE, part * TILE + TILE)
 
-        def edge_row(high, m, c):
+        def edge_row(high, m):
             if part == 0:
-                edge = span_recv[8 * m + high - FIRST_EDGE, c : c + 1, :]
+                edge = span_recv[half, pl.ds(8 * m + high - FIRST_EDGE, 1), :]
                 return jnp.where(ahead, edge, 0.0)
-            if part == 1:
-                return edge_recv[8 * m + high, c : c + 1, :]
-            return recv4[8 * m + high, c, part * TILE - 1 : part * TILE, :]
+            if (half, part) in ((1, 1), (1, 2)):
+                return edge_recv[8 * m + high, part - 1 : part, :]
+            return recv4[8 * m + high, half, part * TILE - 1 : part * TILE, :]
 
         def one_position(high, carry):
             weights = [
-                taps[t : t + 1, pl.ds(pl.multiple_of(high * LANES, LANES), LANES)]
+                half_taps[half, t : t + 1, pl.ds(pl.multiple_of(high * LANES, LANES), LANES)]
                 for t in range(8)
             ]
-            for c in range(2):
-                now = [recv4[8 * m + high, c, at, :] for m in range(16)]
-                old = [None] * 16
-                for m in range(9, 16):
-                    old[m] = jnp.where(first_row, edge_row(high, m, c), pltpu.roll(now[m], 1, 0))
-                for m in range(16):
-                    total = weights[0] * now[m]
-                    for t in range(1, 8):
-                        total = total + weights[t] * (now[m - t] if m >= t else old[m - t + 16])
-                    work[16 * high + m, c, at, :] = total
+            now = [recv4[8 * m + high, half, at, :] for m in range(16)]
+            old = [None] * 16
+            for m in range(9, 16):
+                old[m] = jnp.where(first_row, edge_row(high, m), pltpu.roll(now[m], 1, 0))
+            for m in range(16):
+                total = weights[0] * now[m]
+                for t in range(1, 8):
+                    total = total + weights[t] * (now[m - t] if m >= t else old[m - t + 16])
+                work[16 * high + m, half, at, :] = total
             return carry
 
         lax.fori_loop(0, 8, one_position, 0)
 
-        def one_frame(m, carry):
-            values = small_dft(
-                [(work[16 * high + m, 0, at, :], work[16 * high + m, 1, at, :]) for high in range(8)],
-                -1,
-            )
-            for a, value in enumerate(values):
-                value = times(value, (out_turn[0, a : a + 1, :], out_turn[1, a : a + 1, :]))
-                for c in range(2):
-                    frames[part, a, c, pl.ds(m, TILE, stride=16), :] = value[c]
+        def some_frames(step, carry):
+            ms = [4 * step + n for n in range(4)]
+            given = [[(work[16 * high + m, half, at, :],) for high in range(8)] for m in ms]
+            done = [small_dft(values, -1) for values in given]
+            for m, values in zip(ms, done):
+                for a, value in enumerate(values):
+                    turn = (
+                        out_turn[2 * half, a : a + 1, :],
+                        out_turn[2 * half + 1, a : a + 1, :],
+                    )
+                    frames[part, a, half, pl.ds(m, TILE, stride=16), :] = packed_times(
+                        value[0], turn
+                    )
             return carry
 
-        lax.fori_loop(0, 16, one_frame, 0)
+        lax.fori_loop(0, 4, some_frames, 0)
 
     def ready_copy(part):
         return pltpu.make_async_copy(gathered.at[part], ready.at[part - 1], out_sem.at[part])
@@ -651,11 +734,16 @@
         for p in parts:
             ready_copy(p).start()
 
-    wait_part(recv4, sems4.at[2])
-    filter_part(3)
-    wait_part(recv4, sems4.at[1])
-    filter_part(2)
-    finish_parts((2, 3))
+    for part in (2, 1, 0):
+        wait4(0, part)
+    for part in (3, 2, 1):
+        filter_part(0, part)
+    send_span(1)
+    send4_part(1, 0)
+    span_copies[0].wait_recv()
+    filter_part(0, 0)
+    wait4(1, 2)
+    filter_part(1, 3)
 
     def wait_edges(count):
         ref = edge_recv.at[pl.ds(0, count)]
@@ -663,17 +751,21 @@
 
     pl.when(with_edges)(lambda: wait_edges(DEVICES - FIRST_EDGE - 1))
     pl.when(jnp.logical_not(with_edges))(lambda: wait_edges(DEVICES - FIRST_EDGE))
-    filter_part(1)
+    filter_part(1, 2)
+    finish_parts((2, 3))
+    wait4(1, 1)
+    filter_part(1, 1)
     finish_parts((1,))
-    wait_part(recv4, sems4.at[0])
-    span_copy.wait_recv()
-    filter_part(0)
+    wait4(1, 0)
+    span_copies[1].wait_recv()
+    filter_part(1, 0)
     late_copy = pltpu.make_async_copy(frames.at[0], late, out_sem.at[0])
     late_copy.start()
     for part in range(1, PARTS):
         ready_copy(part).wait()
     late_copy.wait()
-    span_copy.wait_send()
+    for copy in span_copies:
+        copy.wait_send()
 
     def wait_edges_sent():
         ref = edge_recv.at[pl.ds(0, DEVICES - 1)]
@@ -733,33 +825,54 @@
     return high, (matrix - high.astype(np.float32)).astype(BF16)
 
 
+BY_HALVES = np.concatenate([c * LANES + h * HALF + np.arange(HALF) for h in (0, 1) for c in (0, 1)])
+
+
+def beside(matrix):
+    high, low = bf16_halves(matrix)
+    return np.concatenate([high, high, low], axis=1)
+
+
+def above(matrix):
+    high, low = bf16_halves(matrix)
+    return np.concatenate([high, high, low], axis=0)
+
+
 def left_matrix(size, sign):
     c, s = dft_parts(size, sign)
-    high, low = bf16_halves(np.block([[c, -s], [s, c]]))
-    return np.concatenate([high, high, low], axis=1)
+    return np.block([[c, -s], [s, c]])
 
 
 def right_matrix(size, sign, scale=1.0):
     c, s = dft_parts(size, sign, scale)
-    high, low = bf16_halves(np.block([[c, s], [-s, c]]))
-    return np.concatenate([high, high, low], axis=0)
-
-
-def turn_table(rows, cols, whole):
-    product = np.arange(rows)[:, None] * np.arange(cols)[None, :] % whole
-    angle = -2.0 * np.pi * product / whole
+    return np.block([[c, s], [-s, c]])
+
+
+def turn_table(rows, cols, sign):
+    whole = rows * cols
+    angle = sign * 2.0 * np.pi * (np.arange(rows)[:, None] * np.arange(cols)[None, :]) / whole
     return np.stack([np.cos(angle), np.sin(angle)]).astype(np.float32)
+
+
+def packed_table(rows, cols, sign):
+    c, s = turn_table(rows, cols, sign)
+    each = []
+    for half in (slice(0, HALF), slice(HALF, LANES)):
+        each.append(np.concatenate([c[:, half], c[:, half]], axis=1))
+        each.append(np.concatenate([-s[:, half], s[:, half]], axis=1))
+    return np.stack(each)
 
 
 def local(voltage, chirp_phase, filter_taps):
     constants = [
-        left_matrix(ROWS, -1),
-        left_matrix(ROWS, 1),
-        right_matrix(LANES, -1),
-        right_matrix(LANES, 1, 2.0**-LOG_TOTAL),
-        left_matrix(LANES, -1),
-        turn_table(128, LANES, 128 * LANES),
-        turn_table(8, LANES, 8 * LANES),
+        beside(left_matrix(ROWS, -1)),
+        beside(np.concatenate(dft_parts(ROWS, 1), axis=1)),
+        above(right_matrix(LANES, -1)),
+        above(right_matrix(LANES, 1, 2.0**-LOG_TOTAL)[:, BY_HALVES]),
+        beside(left_matrix(LANES, -1)[:, BY_HALVES]),
+        turn_table(128, LANES, -1),
+        packed_table(128, LANES, 1),
+        packed_table(8, LANES, -1),
     ]
     blocks = pltpu.VMEM((DEVICES, 2, ROWS, LANES), F32)
     phases = pltpu.VMEM((DEVICES, ROWS, LANES), F32)
@@ -783,17 +896,18 @@
             pltpu.VMEM((DEVICES, TILE, 2 * LANES), F32),
             pltpu.VMEM((DEVICES, 2, LANES), F32),
             pltpu.VMEM((DEVICES, 2, LANES), F32),
-            pltpu.VMEM((DEVICES - FIRST_EDGE, 2, LANES), F32),
-            pltpu.VMEM((DEVICES - FIRST_EDGE, 2, LANES), F32),
+            pltpu.VMEM((2, DEVICES - FIRST_EDGE, LANES), F32),
+            pltpu.VMEM((2, DEVICES - FIRST_EDGE, LANES), F32),
+            pltpu.VMEM((2, 8, 1024), F32),
             pltpu.SemaphoreType.DMA((2,)),
             pltpu.SemaphoreType.DMA((PARTS,)),
             pltpu.SemaphoreType.DMA((PARTS,)),
-            pltpu.SemaphoreType.DMA((PARTS * GROUPS,)),
-            pltpu.SemaphoreType.DMA((PARTS,)),
+            pltpu.SemaphoreType.DMA((2 * PARTS * GROUPS,)),
+            pltpu.SemaphoreType.DMA((2 * PARTS,)),
             pltpu.SemaphoreType.DMA,
             pltpu.SemaphoreType.DMA,
-            pltpu.SemaphoreType.DMA,
-            pltpu.SemaphoreType.DMA((7,)),
+            pltpu.SemaphoreType.DMA((2,)),
+            pltpu.SemaphoreType.DMA((8,)),
             pltpu.SemaphoreType.DMA((PARTS,)),
             pltpu.SemaphoreType.DMA((CONSTANTS,)),
             pltpu.SemaphoreType.REGULAR,

time: 232 us -> 228 us (0.983)
  Pallas kernels: 232 us -> 227 us
    pallas_call x1, Pallas kernels: 228 us -> 223 us  [local(): pl.pallas_call(kernel, out_shape=[jax.ShapeDtypeStruct((8, 2, 128, LANES)...]
where the time goes in v4:
time: 228 us
  Pallas kernels  227 us (100%)
    pallas_call x1, Pallas kernels, local(): pl.pallas_call(kernel, out_shape=[jax.ShapeDtypeStruct((8, 2, 128, LANES)...  223 us

profile of v4, /device:TPU:1, one launch (start us, length us, event | category | flops | bytes accessed | tf_op | source)
XLA Modules:
  0.0 227.6 jit_solution(11054449052830737939)
XLA Ops:
  0.0 223.4 %shard_map.109 = (f32[8,2,128,128]{3,2,1,0:T(8,128)}, f32[3,2,1024,128]{3,2,1,0:T(8,128)}) custom-call(f32[2,32,16384]{2,1,0:T(8,128)} %voltage.1, f32[128,4096]{1,0:T(8,128)} %phase.1, f32[8,1024]{1,0:T(8,128)} %refs_0_.1, bf16[64,192]{1,0:T(8,128)(2,1)} %constant.16.clone.refs_1_, bf16[32,192]{1,0:T(8,128)(2,1)} %constant.17.clone.refs_2_, ...), custom_call_target="tpu_custom_call" | custom-call | tf_op jit(solution)/shard_map/pallas_call | solution.py:881
  223.4 4.0 %shard_map.110 = f32[2,1024,512]{2,1,0:T(8,128)} custom-call(f32[8,2,128,128]{3,2,1,0:T(8,128)} %get-tuple-element.7.late, f32[3,2,1024,128]{3,2,1,0:T(8,128)} %get-tuple-element.8.ready, bf16[256,768]{1,0:T(8,128)(2,1)} %constant.20.clone.refs_5_.lanes_out), custom_call_target="tpu_custom_call" | custom-call | tf_op jit(solution)/shard_map/pallas_call | solution.py:919

commit v5 on v4

--- a/solution.py
+++ b/solution.py
@@ -267,23 +267,15 @@
     z, y, x, core = place
     barrier = pltpu.get_barrier_semaphore()
 
-    def greet(step, carry):
-        to = device_at(
-            z,
-            lax.rem(y + lax.rem(step, 4), 4),
-            lax.rem(x + lax.rem(step // 4, 4), 4),
-            lax.rem(core + step // 16, 2),
-        )
-        pl.semaphore_signal(barrier, inc=1, device_id=to, device_id_type=BY_MESH)
-        return carry
-
     def greet_along(other):
         to = device_at(lax.rem(z + other, 4), y, x, core)
         return dict(inc=1, device_id=to, device_id_type=BY_MESH)
 
+    for _, dy, dx, dc in (offset for offset in FAR_FIRST if offset[0] == 0):
+        to = device_at(z, lax.rem(y + dy, 4), lax.rem(x + dx, 4), lax.rem(core + dc, 2))
+        pl.semaphore_signal(barrier, inc=1, device_id=to, device_id_type=BY_MESH)
     for other in range(1, 4):
         pl.semaphore_signal(barrier, **greet_along(other))
-    lax.fori_loop(1, 32, greet, 0)
     pl.semaphore_wait(barrier, 34)
     for other in range(1, 4):
         pl.semaphore_signal(plane_sem, **greet_along(other))
@@ -524,24 +516,20 @@
 
             block_dft(load_back, tiles, finish_back, 1)
             recv3[me, half, at, :] = send3[me, half, at, :]
-        send3_part(0, part)
+        send3_rows(0, at, part * GROUPS)
         return carry
 
-    def send3_part(half, part):
+    def send3_rows(half, rows, first_sem):
         send_all(
             IN_STEPS,
-            lambda to: send3.at[to, half, tile_rows(part), :],
-            recv3.at[me, half, tile_rows(part), :],
+            lambda to: send3.at[to, half, rows, :],
+            recv3.at[me, half, rows, :],
             send_sems.at[3],
-            lambda n: sems3.at[(half * PARTS + part) * GROUPS + n // 16],
+            lambda n: sems3.at[first_sem + n // 16],
         )
 
-    def send3_later(part, carry):
-        send3_part(1, part)
-        return carry
-
     lax.fori_loop(0, PARTS, middle_part, 0)
-    lax.fori_loop(0, PARTS, send3_later, 0)
+    send3_rows(1, slice(0, ROWS), PARTS * GROUPS)
 
     def third_step(half, group, eighth):
         places = []
@@ -564,14 +552,18 @@
             work[a, half] = packed_times(value, (table_a[a, 0], -sign * table_a[a, 1]))
 
     def third_group(half, group, count):
+        def wait_rows(rows, sem):
+            ref = recv3.at[pl.ds(0, count), half, pl.ds(0, rows), :]
+            pltpu.make_async_copy(ref, ref, sems3.at[sem + group]).wait()
+
         def wait_one(part, inner):
-            ref = recv3.at[pl.ds(0, count), half, pl.ds(0, TILE), :]
-            pltpu.make_async_copy(
-                ref, ref, sems3.at[(half * PARTS + part) * GROUPS + group]
-            ).wait()
+            wait_rows(TILE, part * GROUPS)
             return inner
 
-        lax.fori_loop(0, PARTS, wait_one, 0)
+        if half == 0:
+            lax.fori_loop(0, PARTS, wait_one, 0)
+        else:
+            wait_rows(ROWS, PARTS * GROUPS)
 
         def one(eighth, inner):
             third_step(half, group, eighth)
@@ -595,20 +587,20 @@
 
         def finish(k, value):
             send4[k, half, at, :] = value[0]
-            if (half, part) in ((1, 0), (1, 1)):
+            if half == 1 and part < 3:
                 edge_send[k, part : part + 1, :] = value[0][TILE - 1 :]
 
         block_dft(load, tiles, finish, 1)
         recv4[me, half, at, :] = send4[me, half, at, :]
 
-    def send4_part(half, part):
-        at = slice(part * TILE, part * TILE + TILE)
+    def send4_tiles(half, first, count):
+        at = slice(first * TILE, (first + count) * TILE)
         send_all(
             FAR_FIRST,
             lambda to: send4.at[to, half, at, :],
             recv4.at[me, half, at, :],
             send_sems.at[4],
-            lambda n: sems4.at[half * PARTS + part],
+            lambda n: sems4.at[half * PARTS + first],
         )
 
     def edge_pieces():
@@ -620,9 +612,9 @@
             lambda n: edge_sem,
         )
 
-    def wait4(half, part):
-        ref = recv4.at[pl.ds(0, DEVICES - 1), half, pl.ds(0, TILE), :]
-        pltpu.make_async_copy(ref, ref, sems4.at[half * PARTS + part]).wait()
+    def wait4(half, first, count):
+        ref = recv4.at[pl.ds(0, DEVICES - 1), half, pl.ds(0, count * TILE), :]
+        pltpu.make_async_copy(ref, ref, sems4.at[half * PARTS + first]).wait()
 
     following = lax.rem(me + 1, DEVICES)
     span_copies = [
@@ -642,24 +634,26 @@
             span_send[half, pl.ds(j, 1), :] = recv4[FIRST_EDGE + j, half, ROWS - 1 :, :]
             return carry
 
-        wait4(half, 3)
         lax.fori_loop(0, DEVICES - FIRST_EDGE, span_row, 0)
         span_copies[half].start()
 
     with_edges = me >= FIRST_EDGE
     third_half(0)
-    for part in (3, 2, 1, 0):
+    fourth_part(0, 3)
+    send4_tiles(0, 3, 1)
+    for part in (2, 1, 0):
         fourth_part(0, part)
-        send4_part(0, part)
+    send4_tiles(0, 0, 3)
     third_half(1)
     for part in (3, 2, 1, 0):
         fourth_part(1, part)
     edge_recv[me] = edge_send[me]
+    wait4(0, 3, 1)
     send_span(0)
-    send4_part(1, 3)
     pl.when(with_edges)(edge_pieces)
-    send4_part(1, 2)
-    send4_part(1, 1)
+    send4_tiles(1, 3, 1)
+    send4_tiles(1, 2, 1)
+    send4_tiles(1, 1, 1)
 
     first_row = lax.broadcasted_iota(jnp.int32, (TILE, LANES), 0) == 0
     ahead = me > 0
@@ -673,7 +667,7 @@
             if part == 0:
                 edge = span_recv[half, pl.ds(8 * m + high - FIRST_EDGE, 1), :]
                 return jnp.where(ahead, edge, 0.0)
-            if (half, part) in ((1, 1), (1, 2)):
+            if half == 1:
                 return edge_recv[8 * m + high, part - 1 : part, :]
             return recv4[8 * m + high, half, part * TILE - 1 : part * TILE, :]
 
@@ -696,7 +690,7 @@
         lax.fori_loop(0, 8, one_position, 0)
 
         def some_frames(step, carry):
-            ms = [4 * step + n for n in range(4)]
+            ms = [8 * step + n for n in range(8)]
             given = [[(work[16 * high + m, half, at, :],) for high in range(8)] for m in ms]
             done = [small_dft(values, -1) for values in given]
             for m, values in zip(ms, done):
@@ -710,7 +704,7 @@
                     )
             return carry
 
-        lax.fori_loop(0, 4, some_frames, 0)
+        lax.fori_loop(0, 2, some_frames, 0)
 
     def ready_copy(part):
         return pltpu.make_async_copy(gathered.at[part], ready.at[part - 1], out_sem.at[part])
@@ -719,31 +713,34 @@
         classes = 2 // len(parts)
 
         def some_classes(step, carry):
-            each = [(p, classes * step + n) for n in range(classes) for p in parts]
-            both = frames_dft(
-                lanes_out, *[jnp.concatenate([frames[p, a, c] for p, a in each]) for c in range(2)]
-            )
-            for c in range(2):
-                for n, (p, a) in enumerate(each):
-                    gathered[p, c, pl.ds(a, 128, stride=8), :] = both[
-                        c * 128 : c * 128 + 128, n * LANES : n * LANES + LANES
-                    ]
+            done = []
+            for group in (2 * step, 2 * step + 1):
+                each = [(p, classes * group + n) for n in range(classes) for p in parts]
+                both = frames_dft(
+                    lanes_out,
+                    *[jnp.concatenate([frames[p, a, c] for p, a in each]) for c in range(2)],
+                )
+                done.append((each, both))
+            for each, both in done:
+                for c in range(2):
+                    for n, (p, a) in enumerate(each):
+                        gathered[p, c, pl.ds(a, 128, stride=8), :] = both[
+                            c * 128 : c * 128 + 128, n * LANES : n * LANES + LANES
+                        ]
             return carry
 
-        lax.fori_loop(0, 8 // classes, some_classes, 0)
+        lax.fori_loop(0, 4 // classes, some_classes, 0)
         for p in parts:
             ready_copy(p).start()
 
-    for part in (2, 1, 0):
-        wait4(0, part)
+    wait4(0, 0, 3)
     for part in (3, 2, 1):
         filter_part(0, part)
+    wait4(1, 3, 1)
     send_span(1)
-    send4_part(1, 0)
+    send4_tiles(1, 0, 1)
     span_copies[0].wait_recv()
     filter_part(0, 0)
-    wait4(1, 2)
-    filter_part(1, 3)
 
     def wait_edges(count):
         ref = edge_recv.at[pl.ds(0, count)]
@@ -751,12 +748,14 @@
 
     pl.when(with_edges)(lambda: wait_edges(DEVICES - FIRST_EDGE - 1))
     pl.when(jnp.logical_not(with_edges))(lambda: wait_edges(DEVICES - FIRST_EDGE))
+    filter_part(1, 3)
+    wait4(1, 2, 1)
     filter_part(1, 2)
     finish_parts((2, 3))
-    wait4(1, 1)
+    wait4(1, 1, 1)
     filter_part(1, 1)
     finish_parts((1,))
-    wait4(1, 0)
+    wait4(1, 0, 1)
     span_copies[1].wait_recv()
     filter_part(1, 0)
     late_copy = pltpu.make_async_copy(frames.at[0], late, out_sem.at[0])
@@ -894,15 +893,15 @@
         + [
             pltpu.VMEM((DEVICES, 2, TILE, LANES), F32),
             pltpu.VMEM((DEVICES, TILE, 2 * LANES), F32),
-            pltpu.VMEM((DEVICES, 2, LANES), F32),
-            pltpu.VMEM((DEVICES, 2, LANES), F32),
+            pltpu.VMEM((DEVICES, 3, LANES), F32),
+            pltpu.VMEM((DEVICES, 3, LANES), F32),
             pltpu.VMEM((2, DEVICES - FIRST_EDGE, LANES), F32),
             pltpu.VMEM((2, DEVICES - FIRST_EDGE, LANES), F32),
             pltpu.VMEM((2, 8, 1024), F32),
             pltpu.SemaphoreType.DMA((2,)),
             pltpu.SemaphoreType.DMA((PARTS,)),
             pltpu.SemaphoreType.DMA((PARTS,)),
-            pltpu.SemaphoreType.DMA((2 * PARTS * GROUPS,)),
+            pltpu.SemaphoreType.DMA(((PARTS + 1) * GROUPS,)),
             pltpu.SemaphoreType.DMA((2 * PARTS,)),
             pltpu.SemaphoreType.DMA,
             pltpu.SemaphoreType.DMA,

time: 228 us -> 227 us (level)
  no operation moved by 1% of the time
where the time goes in v5:
time: 227 us
  Pallas kernels  226 us (100%)
    pallas_call x1, Pallas kernels, local(): pl.pallas_call(kernel, out_shape=[jax.ShapeDtypeStruct((8, 2, 128, LANES)...  222 us

profile of v5, /device:TPU:1, one launch (start us, length us, event | category | flops | bytes accessed | tf_op | source)
XLA Modules:
  0.0 226.5 jit_solution(11036154455934392705)
XLA Ops:
  0.0 222.4 %shard_map.109 = (f32[8,2,128,128]{3,2,1,0:T(8,128)}, f32[3,2,1024,128]{3,2,1,0:T(8,128)}) custom-call(f32[2,32,16384]{2,1,0:T(8,128)} %voltage.1, f32[128,4096]{1,0:T(8,128)} %phase.1, f32[8,1024]{1,0:T(8,128)} %refs_0_.1, bf16[64,192]{1,0:T(8,128)(2,1)} %constant.16.clone.refs_1_, bf16[32,192]{1,0:T(8,128)(2,1)} %constant.17.clone.refs_2_, ...), custom_call_target="tpu_custom_call" | custom-call | tf_op jit(solution)/shard_map/pallas_call | solution.py:880
  222.4 4.0 %shard_map.110 = f32[2,1024,512]{2,1,0:T(8,128)} custom-call(f32[8,2,128,128]{3,2,1,0:T(8,128)} %get-tuple-element.7.late, f32[3,2,1024,128]{3,2,1,0:T(8,128)} %get-tuple-element.8.ready, bf16[256,768]{1,0:T(8,128)(2,1)} %constant.20.clone.refs_5_.lanes_out), custom_call_target="tpu_custom_call" | custom-call | tf_op jit(solution)/shard_map/pallas_call | solution.py:918

commit v6 on v5

--- a/solution.py
+++ b/solution.py
@@ -240,6 +240,7 @@
     span_sems,
     send_sems,
     out_sem,
+    late_sem,
     given_sem,
     plane_sem,
     ) = refs
@@ -587,7 +588,7 @@
 
         def finish(k, value):
             send4[k, half, at, :] = value[0]
-            if half == 1 and part < 3:
+            if half == 1 and part < 2:
                 edge_send[k, part : part + 1, :] = value[0][TILE - 1 :]
 
         block_dft(load, tiles, finish, 1)
@@ -667,7 +668,7 @@
             if part == 0:
                 edge = span_recv[half, pl.ds(8 * m + high - FIRST_EDGE, 1), :]
                 return jnp.where(ahead, edge, 0.0)
-            if half == 1:
+            if half == 1 and part < 3:
                 return edge_recv[8 * m + high, part - 1 : part, :]
             return recv4[8 * m + high, half, part * TILE - 1 : part * TILE, :]
 
@@ -733,6 +734,10 @@
         for p in parts:
             ready_copy(p).start()
 
+    late_copies = [
+        pltpu.make_async_copy(frames.at[0, :, half], late.at[:, half], late_sem.at[half])
+        for half in range(2)
+    ]
     wait4(0, 0, 3)
     for part in (3, 2, 1):
         filter_part(0, part)
@@ -741,6 +746,7 @@
     send4_tiles(1, 0, 1)
     span_copies[0].wait_recv()
     filter_part(0, 0)
+    late_copies[0].start()
 
     def wait_edges(count):
         ref = edge_recv.at[pl.ds(0, count)]
@@ -748,8 +754,8 @@
 
     pl.when(with_edges)(lambda: wait_edges(DEVICES - FIRST_EDGE - 1))
     pl.when(jnp.logical_not(with_edges))(lambda: wait_edges(DEVICES - FIRST_EDGE))
+    wait4(1, 2, 1)
     filter_part(1, 3)
-    wait4(1, 2, 1)
     filter_part(1, 2)
     finish_parts((2, 3))
     wait4(1, 1, 1)
@@ -758,11 +764,11 @@
     wait4(1, 0, 1)
     span_copies[1].wait_recv()
     filter_part(1, 0)
-    late_copy = pltpu.make_async_copy(frames.at[0], late, out_sem.at[0])
-    late_copy.start()
+    late_copies[1].start()
     for part in range(1, PARTS):
         ready_copy(part).wait()
-    late_copy.wait()
+    for copy in late_copies:
+        copy.wait()
     for copy in span_copies:
         copy.wait_send()
 
@@ -778,7 +784,10 @@
 
 
 def last_kernel(late, ready, lanes_out, result, frames, passing, gathered, matrix, sems, more):
-    frame_copies = [pltpu.make_async_copy(late.at[a], frames.at[a], sems.at[a]) for a in range(8)]
+    frame_copies = [
+        pltpu.make_async_copy(late.at[pl.ds(4 * n, 4)], frames.at[pl.ds(4 * n, 4)], sems.at[n])
+        for n in range(2)
+    ]
     matrix_copy = pltpu.make_async_copy(lanes_out, matrix, more.at[0])
     pass_in = [
         pltpu.make_async_copy(ready.at[n], passing.at[n], more.at[1 + n]) for n in range(3)
@@ -793,20 +802,23 @@
     for copy in frame_copies + pass_in:
         copy.start()
     matrix_copy.wait()
-    for a in range(0, 8, 2):
-        frame_copies[a].wait()
-        frame_copies[a + 1].wait()
-        both = frames_dft(
-            matrix, *[jnp.concatenate([frames[a, c], frames[a + 1, c]]) for c in range(2)]
-        )
-        for c in range(2):
-            for n in range(2):
-                gathered[c, pl.ds(a + n, 128, stride=8), :] = both[
-                    c * 128 : c * 128 + 128, n * LANES : n * LANES + LANES
-                ]
-        if a < 6:
-            pass_in[a // 2].wait()
-            passed[a // 2].start()
+    for n in range(2):
+        frame_copies[n].wait()
+        pairs = [(4 * n, 4 * n + 1), (4 * n + 2, 4 * n + 3)]
+        done = [
+            frames_dft(matrix, *[jnp.concatenate([frames[a, c] for a in pair]) for c in range(2)])
+            for pair in pairs
+        ]
+        for pair, both in zip(pairs, done):
+            for c in range(2):
+                for side, a in enumerate(pair):
+                    gathered[c, pl.ds(a, 128, stride=8), :] = both[
+                        c * 128 : c * 128 + 128, side * LANES : side * LANES + LANES
+                    ]
+        if n == 0:
+            for copy_in, copy_out in zip(pass_in, passed):
+                copy_in.wait()
+                copy_out.start()
     computed.start()
     for copy in passed + [computed]:
         copy.wait()
@@ -893,8 +905,8 @@
         + [
             pltpu.VMEM((DEVICES, 2, TILE, LANES), F32),
             pltpu.VMEM((DEVICES, TILE, 2 * LANES), F32),
-            pltpu.VMEM((DEVICES, 3, LANES), F32),
-            pltpu.VMEM((DEVICES, 3, LANES), F32),
+            pltpu.VMEM((DEVICES, 2, LANES), F32),
+            pltpu.VMEM((DEVICES, 2, LANES), F32),
             pltpu.VMEM((2, DEVICES - FIRST_EDGE, LANES), F32),
             pltpu.VMEM((2, DEVICES - FIRST_EDGE, LANES), F32),
             pltpu.VMEM((2, 8, 1024), F32),
@@ -908,6 +920,7 @@
             pltpu.SemaphoreType.DMA((2,)),
             pltpu.SemaphoreType.DMA((8,)),
             pltpu.SemaphoreType.DMA((PARTS,)),
+            pltpu.SemaphoreType.DMA((2,)),
             pltpu.SemaphoreType.DMA((CONSTANTS,)),
             pltpu.SemaphoreType.REGULAR,
         ],

time: 227 us -> 226 us (level)
  no operation moved by 1% of the time
where the time goes in v6:
time: 226 us
  Pallas kernels  226 us (100%)
    pallas_call x1, Pallas kernels, local(): pl.pallas_call(kernel, out_shape=[jax.ShapeDtypeStruct((8, 2, 128, LANES)...  222 us

profile of v6, /device:TPU:1, one launch (start us, length us, event | category | flops | bytes accessed | tf_op | source)
XLA Modules:
  0.0 225.8 jit_solution(4761573325881497342)
XLA Ops:
  0.0 221.6 %shard_map.109 = (f32[8,2,128,128]{3,2,1,0:T(8,128)}, f32[3,2,1024,128]{3,2,1,0:T(8,128)}) custom-call(f32[2,32,16384]{2,1,0:T(8,128)} %voltage.1, f32[128,4096]{1,0:T(8,128)} %phase.1, f32[8,1024]{1,0:T(8,128)} %refs_0_.1, bf16[64,192]{1,0:T(8,128)(2,1)} %constant.16.clone.refs_1_, bf16[32,192]{1,0:T(8,128)(2,1)} %constant.17.clone.refs_2_, ...), custom_call_target="tpu_custom_call" | custom-call | tf_op jit(solution)/shard_map/pallas_call | solution.py:892
  221.6 4.1 %shard_map.110 = f32[2,1024,512]{2,1,0:T(8,128)} custom-call(f32[8,2,128,128]{3,2,1,0:T(8,128)} %get-tuple-element.7.late, f32[3,2,1024,128]{3,2,1,0:T(8,128)} %get-tuple-element.8.ready, bf16[256,768]{1,0:T(8,128)(2,1)} %constant.20.clone.refs_5_.lanes_out), custom_call_target="tpu_custom_call" | custom-call | tf_op jit(solution)/shard_map/pallas_call | solution.py:931

commit v7 on v6

--- a/solution.py
+++ b/solution.py
@@ -649,10 +649,10 @@
     for part in (3, 2, 1, 0):
         fourth_part(1, part)
     edge_recv[me] = edge_send[me]
+    send4_tiles(1, 3, 1)
     wait4(0, 3, 1)
     send_span(0)
     pl.when(with_edges)(edge_pieces)
-    send4_tiles(1, 3, 1)
     send4_tiles(1, 2, 1)
     send4_tiles(1, 1, 1)
 

time: 226 us -> 226 us (level)
  no operation moved by 1% of the time
where the time goes in v7:
time: 226 us
  Pallas kernels  225 us (100%)
    pallas_call x1, Pallas kernels, local(): pl.pallas_call(kernel, out_shape=[jax.ShapeDtypeStruct((8, 2, 128, LANES)...  221 us

profile of v7, /device:TPU:1, one launch (start us, length us, event | category | flops | bytes accessed | tf_op | source)
XLA Modules:
  0.0 225.5 jit_solution(1285866975779982654)
XLA Ops:
  0.0 221.3 %shard_map.109 = (f32[8,2,128,128]{3,2,1,0:T(8,128)}, f32[3,2,1024,128]{3,2,1,0:T(8,128)}) custom-call(f32[2,32,16384]{2,1,0:T(8,128)} %voltage.1, f32[128,4096]{1,0:T(8,128)} %phase.1, f32[8,1024]{1,0:T(8,128)} %refs_0_.1, bf16[64,192]{1,0:T(8,128)(2,1)} %constant.16.clone.refs_1_, bf16[32,192]{1,0:T(8,128)(2,1)} %constant.17.clone.refs_2_, ...), custom_call_target="tpu_custom_call" | custom-call | tf_op jit(solution)/shard_map/pallas_call | solution.py:892
  221.3 4.1 %shard_map.110 = f32[2,1024,512]{2,1,0:T(8,128)} custom-call(f32[8,2,128,128]{3,2,1,0:T(8,128)} %get-tuple-element.7.late, f32[3,2,1024,128]{3,2,1,0:T(8,128)} %get-tuple-element.8.ready, bf16[256,768]{1,0:T(8,128)(2,1)} %constant.20.clone.refs_5_.lanes_out), custom_call_target="tpu_custom_call" | custom-call | tf_op jit(solution)/shard_map/pallas_call | solution.py:931
